TPU v7x, 32 devices: a whole 2x2x4 slice. The times are simulated.
32 devices in a mesh: fsdp: 32 (over z, y, x, core).
Axes of the slice: x: 2, y: 2, z: 4, core: 2. Of those that a mesh axis runs over, the one named last changes fastest.
Arguments:
- timesteps: float32 [16384], P('fsdp')
- guidance: float32 [16384], P('fsdp')
- pooled: bfloat16 [16384, 2048], P('fsdp')
- time_w1: bfloat16 [256, 1152], replicated
- time_b1: bfloat16 [1152], replicated
- time_w2: bfloat16 [1152, 1152], replicated
- time_b2: bfloat16 [1152], replicated
- guide_w1: bfloat16 [256, 1152], replicated
- guide_b1: bfloat16 [1152], replicated
- guide_w2: bfloat16 [1152, 1152], replicated
- guide_b2: bfloat16 [1152], replicated
- text_w1: bfloat16 [2048, 1152], replicated
- text_b1: bfloat16 [1152], replicated
- text_w2: bfloat16 [1152, 1152], replicated
- text_b2: bfloat16 [1152], replicated
- w_mod: bfloat16 [1152, 5760], P(None, 'fsdp')
- b_mod: bfloat16 [5760], P('fsdp')
- d_mods: bfloat16 [16384, 5760], P('fsdp')
Outputs:
- output 1: bfloat16 [16384, 5760], P('fsdp')
- output 2: float32 [1152, 5760], P(None, 'fsdp')
- output 3: float32 [5760], P('fsdp')
- output 4: float32 [256, 1152], replicated
- output 5: float32 [1152], replicated
- output 6: float32 [1152, 1152], replicated
- output 7: float32 [1152], replicated
- output 8: float32 [256, 1152], replicated
- output 9: float32 [1152], replicated
- output 10: float32 [1152, 1152], replicated
- output 11: float32 [1152], replicated
- output 12: float32 [2048, 1152], replicated
- output 13: float32 [1152], replicated
- output 14: float32 [1152, 1152], replicated
- output 15: float32 [1152], replicated
All inputs are finite; a program needn't handle non-finite values.
Results may differ from a plain program's by a relative error of at most 0.00486957.
Values are sent between devices in bfloat16 or wider.
A program may use at most 1 GiB of HBM per device.

v0:
```python
import math
import jax
import jax.numpy as jnp
from jax import lax
from jax.sharding import PartitionSpec as P

MESH_AXIS = "fsdp"
MAX_PERIOD = 10000.0
TIME_SCALE = 1000.0
CONTRACT_ROWS = (((0,), (0,)), ((), ()))
CONTRACT_COLS = (((1,), (1,)), ((), ()))


def sinusoid(values, freq_width):
    half_width = freq_width // 2
    freq_table = jnp.exp(-math.log(MAX_PERIOD) * jnp.arange(half_width, dtype=jnp.float32) / half_width)
    angles = (TIME_SCALE * values)[:, None] * freq_table[None, :]
    return jnp.concatenate([jnp.cos(angles), jnp.sin(angles)], axis=1).astype(jnp.bfloat16)


def silu_grad(values):
    sigmoid_v = jax.nn.sigmoid(values)
    return sigmoid_v * (1.0 + values * (1.0 - sigmoid_v))


def mlp_forward(inputs_bf, params):
    hidden = jnp.dot(inputs_bf, params[0], preferred_element_type=jnp.float32) + params[1].astype(jnp.float32)
    act_bf = jax.nn.silu(hidden).astype(jnp.bfloat16)
    output = jnp.dot(act_bf, params[2], preferred_element_type=jnp.float32) + params[3].astype(jnp.float32)
    return output, hidden, act_bf


def mlp_backward(inputs_bf, params, hidden, act_bf, d_out, d_out_bf):
    grad_w2 = lax.dot_general(act_bf, d_out_bf, CONTRACT_ROWS, preferred_element_type=jnp.float32)
    grad_b2 = jnp.sum(d_out, axis=0)
    d_act = lax.dot_general(d_out_bf, params[2], CONTRACT_COLS, preferred_element_type=jnp.float32)
    d_hidden = d_act * silu_grad(hidden)
    grad_w1 = lax.dot_general(inputs_bf, d_hidden.astype(jnp.bfloat16), CONTRACT_ROWS, preferred_element_type=jnp.float32)
    grad_b1 = jnp.sum(d_hidden, axis=0)
    return (grad_w1, grad_b1, grad_w2, grad_b2)


def embed_forward(inputs_list, params_list):
    saved_acts = [mlp_forward(inputs_bf, params) for inputs_bf, params in zip(inputs_list, params_list)]
    cond_vec = saved_acts[0][0] + saved_acts[1][0] + saved_acts[2][0]
    return cond_vec, saved_acts


def embed_backward(inputs_list, params_list, saved_acts, d_vec):
    d_vec_bf = d_vec.astype(jnp.bfloat16)
    grad_list = []
    for inputs_bf, params, record in zip(inputs_list, params_list, saved_acts):
        grad_list.extend(mlp_backward(inputs_bf, params, record[1], record[2], d_vec, d_vec_bf))
    return tuple(grad_list)


def solution(mesh):
    row_split = P(MESH_AXIS)
    row_matrix = P(MESH_AXIS, None)
    col_matrix = P(None, MESH_AXIS)
    embed_specs = (P(None, None), P(None), P(None, None), P(None)) * 3
    in_specs = (row_split, row_split, row_matrix) + embed_specs + (col_matrix, row_split, row_matrix)
    out_specs = (row_matrix, col_matrix, row_split) + embed_specs

    def local_step(timesteps, guidance, pooled, time_w1, time_b1, time_w2, time_b2, guide_w1, guide_b1, guide_w2, guide_b2, text_w1, text_b1, text_w2, text_b2, w_mod, b_mod, d_mods):
        freq_width = time_w1.shape[0]
        inputs_list = [sinusoid(timesteps, freq_width), sinusoid(guidance, freq_width), pooled]
        params_list = [(time_w1, time_b1, time_w2, time_b2), (guide_w1, guide_b1, guide_w2, guide_b2), (text_w1, text_b1, text_w2, text_b2)]
        cond_vec, saved_acts = embed_forward(inputs_list, params_list)
        cond_silu = jax.nn.silu(cond_vec).astype(jnp.bfloat16)
        full_wmod = lax.all_gather(w_mod, MESH_AXIS, axis=1, tiled=True)
        full_bmod = lax.all_gather(b_mod, MESH_AXIS, axis=0, tiled=True)
        modulation = (jnp.dot(cond_silu, full_wmod, preferred_element_type=jnp.float32) + full_bmod.astype(jnp.float32)).astype(jnp.bfloat16)
        part_wgrad = lax.dot_general(cond_silu, d_mods, CONTRACT_ROWS, preferred_element_type=jnp.float32)
        grad_wmod = lax.psum_scatter(part_wgrad, MESH_AXIS, scatter_dimension=1, tiled=True)
        part_bgrad = jnp.sum(d_mods, axis=0, dtype=jnp.float32)
        grad_bmod = lax.psum_scatter(part_bgrad, MESH_AXIS, scatter_dimension=0, tiled=True)
        d_cond = lax.dot_general(d_mods, full_wmod, CONTRACT_COLS, preferred_element_type=jnp.float32)
        d_vec = d_cond * silu_grad(cond_vec)
        embed_grads = lax.psum(embed_backward(inputs_list, params_list, saved_acts, d_vec), MESH_AXIS)
        return (modulation, grad_wmod, grad_bmod) + tuple(embed_grads)

    return jax.shard_map(local_step, mesh=mesh, in_specs=in_specs, out_specs=out_specs, check_vma=False)
```

profile of v0, /device:TPU:0, one launch (start us, length us, event | category | flops | bytes accessed | tf_op | source)
XLA Modules:
  0.0 811.1 jit_solution(14643214851071449613)
XLA Ops:
  7.2 0.7 all-gather.3.cloned.1.call-update
  8.0 0.8 convert_element_type.55
  8.7 0.7 convert_element_type.53
  9.4 0.7 convert_element_type.58
  10.1 0.7 convert_element_type.56
  10.8 0.7 convert_element_type.61
  11.5 0.7 convert_element_type.59
  12.2 0.7 broadcast_multiply_fusion
  12.9 2.2 fusion.10
  15.1 1.6 convolution_add_fusion.1
  17.2 0.9 copy-done.2
  18.1 2.1 convolution_add_fusion.5
  20.7 2.1 fusion.2
  22.9 2.9 convolution_add_fusion.3
  25.8 1.4 copy-done.18
  27.2 3.5 fusion.1
  30.7 83.0 %all-gather.3.cloned.1.call-done = bf16[32,180,1152]{2,1,0:T(8,128)(2,1)} async-done(((bf16[1,180,1152]{2,1,0:T(8,128)(2,1)}), bf16[32,180,1152]{2,1,0:T(8,128)(2,1)}) %all-gather.3.cloned.1.call-update) | async-done | bytes 13271056 | tf_op jit(solution)/shard_map/all_gather | solution.py:71
  113.7 16.3 %reshape.47 = bf16[5760,1152]{1,0:T(8,128)(2,1)} reshape(bf16[32,180,1152]{2,1,0:T(8,128)(2,1)} %all-gather.3.cloned.1.call-done) | data formatting | bytes 26542080
  130.0 24.3 %fusion.20 = (f32[1152]{0:T(1024)S(1)}, bf16[512,1152]{1,0:T(8,128)(2,1)S(1)}) fusion(f32[512,1152]{1,0:T(8,128)} %fusion.1, bf16[512,5760]{1,0:T(8,128)(2,1)} %param.35, bf16[5760,1152]{1,0:T(8,128)(2,1)} %reshape.47), kind=kOutput, calls=%fused_computation.50 | convolution fusion | flops 6800669696 | bytes 22712832 | tf_op jit(solution)/shard_map/dot_general | solution.py:78
  154.4 2.0 fusion.21
  156.9 2.0 fusion.22
  159.3 2.0 fusion.23
  161.3 4.2 fusion.16
  165.5 4.2 fusion.17
  169.7 4.2 fusion.18
  173.8 1.5 fusion.6
  175.4 1.5 fusion.4
  176.9 5.2 convolution_bitcast_fusion
  182.1 1.6 copy-done.17
  183.8 16.3 %fusion.19 = f32[1152,5760]{0,1:T(8,128)} fusion(bf16[512,5760]{1,0:T(8,128)(2,1)} %param.35, f32[512,1152]{1,0:T(8,128)S(1)} %copy-done.17), kind=kOutput, calls=%fused_computation.49 | convolution fusion | flops 6797721600 | bytes 34799616 | tf_op jit(solution)/shard_map/dot_general | solution.py:74
  200.1 365.8 %fusion = f32[1152,192]{0,1:T(8,128)S(1)} fusion(f32[1152,5760]{0,1:T(8,128)} %fusion.19), kind=kCustom, calls=%all-reduce-scatter | all-reduce-scatter fusion | flops 7077889 | bytes 27426816
  565.9 13.3 %collective-permute-start = (f32[1152,192]{0,1:T(8,128)S(1)}, f32[1152,192]{0,1:T(8,128)S(1)}, u32[]{:S(2)}, u32[]{:S(2)}) collective-permute-start(f32[1152,192]{0,1:T(8,128)S(1)} %fusion), channel_id=1, source_target_pairs={{0,1},{1,2},{2,3},{3,4},{4,5},{5,6},{6,7},{7,8},{8,9},{9,10},{10,1... | collective-permute-start | bytes 2654216
  579.3 4.3 collective-permute-start.1
  583.9 78.3 %all-reduce = bf16[5760]{0:T(1024)(128)(2,1)S(1)} all-reduce(bf16[5760]{0:T(1024)(128)(2,1)S(1)} %dynamic-update-slice), channel_id=1, replica_groups=mesh['fsdp'=32] {'fsdp'}, use_global_device_ids=true, to_apply=%add | all-reduce | flops 5760 | bytes 23040
  662.2 4.0 convert_reduce_fusion
  666.2 7.8 concatenate.10
  674.0 2.1 constant_dynamic-slice_fusion
  676.1 42.4 %all-reduce.4 = (f32[5760]{0:T(1024)S(1)}, f32[1152]{0:T(1024)}, f32[1152]{0:T(1024)S(1)}, f32[1152]{0:T(1024)}, f32[1152]{0:T(1024)}) all-reduce(f32[5760]{0:T(1024)S(1)} %convert_reduce_fusion, f32[1152]{0:T(1024)S(1)} %get-tuple-element.80, f32[1152]{0:T(1024)S(1)} %get-tuple-element.71, ...), channel_id=3, replica_groups=mesh['fsdp'=32] {'fsdp'}, use_global_device_ids=true, to_apply=%region_2.3.clone | all-reduce | flops 10368 | bytes 82944
  719.1 15.1 %add_convert_fusion = bf16[512,5760]{1,0:T(8,128)(2,1)} fusion(bf16[5760,1152]{1,0:T(8,128)(2,1)} %reshape.47, f32[5760]{0:T(1024)S(1)} %convert_element_type.63, f32[512,1152]{1,0:T(8,128)} %fusion.1), kind=kOutput, calls=%fused_computation.1 | convolution fusion | flops 6803619840 | bytes 21551616 | tf_op jit(solution)/shard_map/dot_general | solution.py:73
  734.2 42.8 %all-reduce.8.cloned.1.call-done = (f32[256,1152]{1,0:T(8,128)}, f32[1152,1152]{1,0:T(8,128)}, f32[256,1152]{1,0:T(8,128)}, f32[1152,1152]{1,0:T(8,128)}, f32[2048,1152]{0,1:T(8,128)}, /*index=5*/f32[1152,1152]{1,0:T(8,128)}) async-done(((f32[256,1152]{1,0:T(8,128)}, f32[1152,1152]{1,0:T(8,128)}, f32[256,1152]{1,0:T(8,128)}, f32[1152,1152]{1,0:T(8,128)}, f32[2048,1152]{0,1:T(8,128)}, ...) | async-done | bytes 27721744 | tf_op jit(solution)/shard_map/psum | solution.py:80
  777.0 9.7 %copy.35 = f32[2048,1152]{1,0:T(8,128)} copy(f32[2048,1152]{0,1:T(8,128)} %get-tuple-element.69) | data formatting | bytes 18874368
  787.9 1.0 copy.47
  788.9 6.2 copy.48
  795.2 1.0 copy.49
  796.2 2.7 copy.50
  799.4 0.8 slice-done.1
  800.2 2.7 copy.51
  802.9 1.0 copy-done.1
  (64 shorter events, 4.9 us)
Async XLA Ops:
  7.2 10.9 %copy-start = (bf16[1152,1152]{1,0:T(8,128)(2,1)S(1)}, bf16[1152,1152]{1,0:T(8,128)(2,1)}, u32[]{:S(2)}) copy-start(bf16[1152,1152]{1,0:T(8,128)(2,1)} %param.23) | copy-start | bytes 7962628
  7.2 106.5 %all-gather.3.cloned.1.call-start = ((), (), s32[]{:S(2)}) async-start(), calls=%async_computation | async-start | bytes 13989888 | tf_op jit(solution)/shard_map/all_gather | solution.py:71
  7.9 769.1 %all-reduce.8.cloned.1.call-start = ((), (), s32[]{:S(2)}) async-start(), calls=%async_computation.1 | async-start | bytes 55443456 | tf_op jit(solution)/shard_map/psum | solution.py:80
  8.0 8.7 %copy-start.8 = (bf16[256,1152]{1,0:T(8,128)(2,1)S(1)}, bf16[256,1152]{1,0:T(8,128)(2,1)}, u32[]{:S(2)}) copy-start(bf16[256,1152]{1,0:T(8,128)(2,1)} %param.25) | copy-start | bytes 1769476
  16.7 1.4 copy-start.2
  18.1 2.1 copy-start.4
  18.1 2.6 copy-start.10
  18.1 4.7 slice-start.4
  20.7 2.1 slice-start.5
  20.7 2.2 copy-start.14
  22.9 4.3 copy-start.12
  25.8 1.4 copy-start.18
  130.0 24.4 %copy-start.3 = (f32[512,1152]{1,0:T(8,128)S(1)}, f32[512,1152]{1,0:T(8,128)}, u32[]{:S(2)}) copy-start(f32[512,1152]{1,0:T(8,128)} %copy-done.2) | copy-start | bytes 7077892
  154.4 2.0 copy-start.5
  154.4 2.5 copy-start.11
  156.8 2.0 copy-start.13
  156.9 2.5 copy-start.19
  173.8 3.1 copy-start.15
  182.1 1.7 copy-start.17
  200.1 383.5 %copy-start.16 = (bf16[180]{0:T(256)(128)(2,1)S(1)}, bf16[180]{0:T(256)(128)(2,1)}, u32[]{:S(2)}) copy-start(bf16[180]{0:T(256)(128)(2,1)} %param.34) | copy-start | bytes 1084
  565.9 100.3 %collective-permute-start = (f32[1152,192]{0,1:T(8,128)S(1)}, f32[1152,192]{0,1:T(8,128)S(1)}, u32[]{:S(2)}, u32[]{:S(2)}) collective-permute-start(f32[1152,192]{0,1:T(8,128)S(1)} %fusion), channel_id=1, source_target_pairs={{0,1},{1,2},{2,3},{3,4},{4,5},{5,6},{6,7},{7,8},{8,9},{9,10},{10,1... | collective-permute-start | bytes 2654216
  579.3 86.9 %collective-permute-start.1 = (f32[1152,180]{0,1:T(8,128)S(1)}, f32[1152,180]{0,1:T(8,128)S(1)}, u32[]{:S(2)}, u32[]{:S(2)}) collective-permute-start(f32[1152,180]{0,1:T(8,128)S(1)} %slice), channel_id=1, source_target_pairs={{0,2},{1,3},{2,4},{3,5},{4,6},{5,7},{6,8},{7,9},{8,10},{9,11},{10,... | collective-permute-start | bytes 2488328
  718.5 68.8 %copy-start.9 = (f32[1152]{0:T(1024)}, f32[1152]{0:T(1024)S(1)}, u32[]{:S(2)}) copy-start(f32[1152]{0:T(1024)S(1)} %get-tuple-element.130) | copy-start | bytes 13828
  777.0 10.9 %copy-start.7 = (f32[256,1152]{1,0:T(8,128)S(1)}, f32[256,1152]{1,0:T(8,128)}, u32[]{:S(2)}) copy-start(f32[256,1152]{1,0:T(8,128)} %get-tuple-element.127) | copy-start | bytes 3538948
  787.9 8.3 %slice-start.2 = ((s8[5308416]{0:T(1024)(128)(4,1)}), s8[4194304]{0:T(1024)(128)(4,1)S(1)}, s32[]{:S(2)}) async-start(s8[5308416]{0:T(1024)(128)(4,1)} %bitcast.31), calls=%async_computation.4 | async-start | bytes 8388608
  788.9 6.3 copy-start.6
  788.9 7.3 slice-start.3
  795.2 4.2 slice-start
  796.2 4.0 slice-start.1
  800.2 3.7 copy-start.1
Sparse Core Ops, SparseCore 0:
  10.9 102.7 all-gather.2
  182.2 594.7 all-reduce.7
where the time goes:
time: 814 us; the launch traced here: 811 us
  blocking collectives  486 us (60%)
  waiting for transfers between devices  127 us (16%)
  matrix products  95.1 us (12%)
  local copies, waits for them, and re-layouts  59.5 us (7%)
  starting transfers between devices  17.7 us (2%)
  between operations  14.8 us (2%)
  other arithmetic  11.1 us (1%)
    unnamed x3, blocking collectives  486 us
    all_gather x1, waiting for transfers between devices, local_step(): full_wmod = lax.all_gather(w_mod, MESH_AXIS, axis=1, tiled=True)  83 us
    unnamed x67, local copies, waits for them, and re-layouts  59.5 us
    psum x1, waiting for transfers between devices, local_step(): lax.psum(embed_backward(inputs_list, params_list, saved_acts, d_vec), MES...  42.8 us
    dot_general x1, matrix products, local_step(): lax.dot_general(d_mods, full_wmod, CONTRACT_COLS, preferred_element_type=...  24.3 us
    unnamed x2, starting transfers between devices  17.6 us
    dot_general x1, matrix products, local_step(): lax.dot_general(cond_silu, d_mods, CONTRACT_ROWS, preferred_element_type=...  16.3 us
  transfers between devices with their start and end apart: 4, of which 2 were waited for; matrix products, arithmetic and copies ran while one was open for 53% of the time, Pallas kernels for 0%

commit v1 on v0

v1 whole, which is shorter than its diff:
```python
import functools
import math
import jax
import jax.numpy as jnp
from jax import lax
from jax.experimental import pallas as pl
from jax.experimental.pallas import tpu as pltpu
from jax.sharding import PartitionSpec as P

AXIS = "fsdp"
MESH = pl.DeviceIdType.MESH
MAX_PERIOD = 10000.0
TIME_SCALE = 1000.0
CONTRACT_ROWS = (((0,), (0,)), ((), ()))
CONTRACT_COLS = (((1,), (1,)), ((), ()))
F32, BF16 = jnp.float32, jnp.bfloat16
VMEM_LIMIT = 62 << 20
TWO, ZS, CHIPS, DEVICES = 2, 4, 16, 32
ROWS, WIDTH, MOD, SHARE, PADDED = 512, 1152, 5760, 180, 184
TILE, TILES = 384, 15
Z_ORDER = (3, 0, 2, 1)
ANY = pl.BlockSpec(memory_space=pl.ANY)
IN_VMEM = pl.BlockSpec(memory_space=pltpu.VMEM)
DMA = pltpu.SemaphoreType.DMA
WMOD_SPLIT = (80, 64, 16, 24)
WGRAD_SPLIT = (72, 72, 24, 16)
EMBED_SPLIT = (80, 72, 24, 16)


class Peers:
    def __init__(self):
        me = lax.axis_index(AXIS)
        bits = []
        for _ in range(3):
            bits.append(lax.rem(me, TWO))
            me = lax.div(me, TWO)
        self.c, self.x, self.y = bits
        self.oc, self.ox, self.oy = (1 - bit for bit in bits)
        self.z = me
        self.core = self.device(me, self.y, self.x, self.oc)
        self.xn = self.device(me, self.y, self.ox, self.c)
        self.yn = self.device(me, self.oy, self.x, self.c)

    def device(self, z, y, x, c):
        return (((z * TWO + y) * TWO + x) * TWO + c,)

    def column(self, zp):
        return self.device(zp, self.y, self.x, self.c)

    def elsewhere(self, fn):
        for zp in range(ZS):
            pl.when(self.z != zp)(functools.partial(fn, zp))

    def barrier(self):
        sem = pltpu.get_barrier_semaphore()

        def greet(peer):
            pl.semaphore_signal(sem, device_id=peer, device_id_type=MESH)

        for peer in (self.core, self.xn, self.yn):
            greet(peer)
        self.elsewhere(lambda zp: greet(self.column(zp)))
        pl.semaphore_wait(sem, 6)


def remote(src, dst, sems, peer):
    pltpu.make_async_remote_copy(src_ref=src, dst_ref=dst, send_sem=sems[0], recv_sem=sems[1], device_id=peer, device_id_type=MESH).start()


def local(src, dst, sem):
    pltpu.make_async_copy(src, dst, sem).start()


def wait_for(ref, sem):
    pltpu.make_async_copy(ref, ref, sem).wait()


def add_rows(dst, src):
    if len(dst.shape) > TWO:
        for i in range(dst.shape[0]):
            add_rows(dst.at[i], src.at[i])
        return
    rows = dst.shape[0]
    step = 24 if rows % 24 == 0 else 8

    def body(i, carry):
        at = pl.ds(pl.multiple_of(i * step, 8), step)
        dst[at, :] = dst[at, :] + src[at, :]
        return carry

    lax.fori_loop(0, rows // step, body, 0)


class Sems:
    def __init__(self, refs, *index):
        self.send, self.recv, self.index = *refs, index

    def __getitem__(self, k):
        return self.send.at[(*self.index, k)], self.recv.at[(*self.index, k)]

    def under(self, k):
        return Sems((self.send, self.recv), *self.index, k)

    @staticmethod
    def scratch(*shape):
        return [DMA(shape), DMA(shape)]


class Split:
    def __init__(self, *n):
        starts = [sum(n[:i]) for i in range(ZS)]
        ranges = [pl.ds(start, size) for start, size in zip(starts, n)]
        self.n, self.colours = (n[:TWO], n[TWO:]), (ranges[:TWO], ranges[TWO:])
        self.a, self.b = sum(self.n[0]), sum(self.n[1])
        self.rows = self.a + self.b
        self.all_a, self.all_b = pl.ds(0, self.a), pl.ds(self.a, self.b)
        size = -(-self.a // DEVICES) * 8
        self.chunks = [pl.ds(at, min(size, self.a - at)) for at in range(0, self.a, size)]


class PlaneReduce:
    @staticmethod
    def shapes(sizes):
        one, two = sizes
        return [(TWO, one), (TWO, two), (one,), (two,)]

    def __init__(self, p, plane, colours, boxes, sems):
        one, two = colours
        x1, y1, y2, x2 = boxes
        self.sems = sems
        self.moves = (
            (plane.at[:, p.ox, one], x1, p.xn), (plane.at[p.oy, :, two], y1, p.yn),
            (plane.at[p.oy, p.x, one], y2, p.yn), (plane.at[p.y, p.ox, two], x2, p.xn),
        )
        mine = plane.at[p.y, p.x]
        self.first = ((x1.at[p.oy], x1.at[p.y]), (y1.at[p.ox], y1.at[p.x]))
        self.mine = (mine.at[one], mine.at[two])

    def send(self, k):
        src, dst, peer = self.moves[k]
        remote(src, dst, self.sems[k], peer)

    def got(self, k):
        wait_for(self.moves[k][1], self.sems[k][1])

    def start(self):
        for k in range(TWO):
            self.send(k)

    def middle(self):
        for k in range(TWO):
            self.got(k)
            add_rows(self.moves[k + TWO][0], self.first[k][0])
            self.send(k + TWO)
        for k in range(TWO):
            add_rows(self.mine[k], self.first[k][1])

    def end(self):
        for k in range(TWO):
            self.got(k + TWO)
            add_rows(self.mine[k], self.moves[k + TWO][1])

    def drain(self):
        for k, move in enumerate(self.moves):
            wait_for(move[1], self.sems[k][0])


class ReduceScatter:
    @staticmethod
    def scratch(s):
        whole = [(ZS, TWO, TWO, s.rows)] * TWO
        planes = [(ZS,) + shape for shape in PlaneReduce.shapes(s.n[0])] + PlaneReduce.shapes(s.n[1])
        shapes = whole + planes + [(TWO, ZS, s.a), (ZS, TWO, TWO, s.b)]
        buffers = [pltpu.VMEM(shape + (WIDTH,), F32) for shape in shapes]
        return buffers + [DMA((ZS,))] + Sems.scratch(ZS) + Sems.scratch(ZS, ZS) + Sems.scratch(TWO, ZS, len(s.chunks)) + Sems.scratch(ZS) + Sems.scratch(ZS)

    def __init__(self, p, sources, pieces, s, scratch):
        self.p, self.sources, self.pieces, self.s = p, sources, pieces, s
        scratch = list(scratch)
        take = lambda n: [scratch.pop(0) for _ in range(n)]
        self.part, self.fromc = take(TWO)
        boxes, slab_boxes = take(ZS), take(ZS)
        self.line, self.slabs, self.lsem = take(3)
        self.csems, plane_sems, self.zsems, self.bsems, slab_sems = (Sems(take(TWO)) for _ in range(5))
        self.planes = [PlaneReduce(p, self.part.at[zp], s.colours[0], [box.at[zp] for box in boxes], plane_sems.under(zp)) for zp in range(ZS)]
        self.slab = PlaneReduce(p, self.part.at[p.z], s.colours[1], slab_boxes, slab_sems)

    def begin(self, zp):
        p = self.p

        def load(core):
            mine = self.pieces[core]
            for src, start, n, at in self.pieces[1 - core]:
                remote(self.sources[src].at[zp, :, :, pl.ds(start, n)], self.fromc.at[zp, :, :, pl.ds(at, n)], self.csems[zp], p.core)
            for src, start, n, at in mine:
                local(self.sources[src].at[zp, :, :, pl.ds(start, n)], self.part.at[zp, :, :, pl.ds(at, n)], self.lsem.at[zp])

        for core in range(TWO):
            pl.when(p.c == core)(functools.partial(load, core))

    def both_cores(self, zp):
        wait_for(self.part.at[zp], self.lsem.at[zp])
        wait_for(self.fromc.at[zp], self.csems[zp][1])
        add_rows(self.part.at[zp], self.fromc.at[zp])

    def slab_out(self, zp):
        p = self.p

        @pl.when(p.z != zp)
        def _():
            sems = self.bsems[zp][0], self.bsems[p.z][1]
            remote(self.part.at[zp, :, :, self.s.all_b], self.slabs.at[p.z], sems, p.column(zp))

    def slab_sum(self, zp):
        wait_for(self.slabs.at[zp], self.bsems[zp][1])
        add_rows(self.part.at[self.p.z, :, :, self.s.all_b], self.slabs.at[zp])

    def line_in(self, way, zp, k, part):
        box = self.line.at[way, zp, part]
        wait_for(box, self.zsems.under(way).under(zp)[k][1])
        add_rows(self.part.at[zp, self.p.y, self.p.x, part], box)

    def hop(self, zp, distance):
        p = self.p

        def go(way, step):
            for k, part in enumerate(self.s.chunks):
                if distance:
                    self.line_in(way, zp, k, part)
                remote(self.part.at[zp, p.y, p.x, part], self.line.at[way, zp, part], self.zsems.under(way).under(zp)[k], p.column(p.z + step))

        last = ZS - 1
        for way, (step, at, todo) in enumerate(((1, distance, distance < zp), (-1, last - distance, last - distance > zp))):
            if todo:
                pl.when(p.z == at)(functools.partial(go, way, step))

    def final(self, zp):
        @pl.when(self.p.z == zp)
        def _():
            for k, part in enumerate(self.s.chunks):
                for way, end in enumerate((0, ZS - 1)):
                    if zp != end:
                        self.line_in(way, zp, k, part)

    def drain(self):
        p = self.p
        self.slab.drain()
        p.elsewhere(lambda zp: wait_for(self.slabs.at[zp], self.bsems[zp][0]))

        def sent(way, zp):
            for k, part in enumerate(self.s.chunks):
                wait_for(self.line.at[way, zp, part], self.zsems.under(way).under(zp)[k][0])

        for zp in range(ZS):
            wait_for(self.fromc.at[zp], self.csems[zp][0])
            self.planes[zp].drain()
            for way, cond in enumerate((p.z < zp, p.z > zp)):
                pl.when(cond)(functools.partial(sent, way, zp))

    def run(self, fill=lambda: None):
        one, two, three, four = Z_ORDER
        planes = self.planes
        for zp in Z_ORDER:
            self.begin(zp)
        for zp in Z_ORDER:
            self.both_cores(zp)
            if zp in (one, two):
                planes[zp].start()
            self.slab_out(zp)
        fill()
        planes[one].middle()
        planes[three].start()
        fill()
        planes[one].end()
        self.hop(one, 0)
        fill()
        planes[two].middle()
        planes[four].start()
        fill()
        planes[two].end()
        self.hop(two, 0)
        self.hop(one, 1)
        fill()
        planes[three].middle()
        fill()
        planes[three].end()
        self.hop(three, 0)
        self.hop(two, 1)
        self.hop(one, TWO)
        fill()
        self.p.elsewhere(self.slab_sum)
        self.slab.start()
        planes[four].middle()
        self.slab.middle()
        planes[four].end()
        self.hop(four, 0)
        self.hop(three, 1)
        self.hop(two, TWO)
        self.hop(four, 1)
        self.slab.end()
        for zp in Z_ORDER:
            self.final(zp)


class PlaneGather:
    def __init__(self, p, plane, colours, sems):
        one, two = colours
        mine, ynb, xnb, far = (plane.at[y, x, p.c] for y, x in ((p.y, p.x), (p.oy, p.x), (p.y, p.ox), (p.oy, p.ox)))
        self.mine, self.blocks, self.sems = mine, (ynb, xnb, far), sems
        self.moves = ((mine, one, p.yn), (mine, two, p.xn), (mine, two, p.yn), (mine, one, p.xn), (ynb, one, p.xn), (xnb, two, p.yn))

    def send(self, k, src=None):
        block, at, peer = self.moves[k]
        remote((block if src is None else src).at[at], block.at[at], self.sems[k], peer)

    def got(self, k, side=1):
        block, at, peer = self.moves[k]
        wait_for(block.at[at], self.sems[k][side])

    def start(self, src):
        for k in range(ZS):
            self.send(k, src)

    def relay(self):
        for k in range(TWO):
            self.got(k)
            self.send(k + ZS)

    def rest(self, forward=None):
        waits = ((TWO,), (3,), (ZS, 5))
        for ks, block in zip(waits, self.blocks):
            for k in ks:
                self.got(k)
            if forward is not None:
                forward(block)

    def drain(self):
        for k in range(len(self.moves)):
            self.got(k, 0)


class AllGather:
    scratch = [*Sems.scratch(TWO, ZS), *Sems.scratch(ZS, 6), *Sems.scratch(ZS), *Sems.scratch(ZS), *Sems.scratch(6), DMA]

    def __init__(self, p, own, out, s, scratch):
        self.p, self.own, self.out, self.s = p, own, out, s
        *pairs, self.lsem = scratch
        self.zsems, self.plane_sems, self.csems, self.bsems, slab_sems = (Sems(pair) for pair in zip(pairs[::TWO], pairs[1::TWO]))
        self.slab = PlaneGather(p, out.at[p.z], s.colours[1], slab_sems)

    def plane(self, zp):
        return PlaneGather(self.p, self.out.at[zp], self.s.colours[0], self.plane_sems.under(zp))

    def band(self, zp):
        return self.out.at[zp, :, :, self.p.c, self.s.all_b]

    def forward(self, zp, src, dst):
        remote(src, dst, self.csems[zp], self.p.core)

    def spread(self, zp, src):
        plane, a = self.plane(zp), self.s.all_a
        plane.start(src)
        self.forward(zp, src.at[a], plane.mine.at[a])

    def send_z(self, way, zp, src):
        p = self.p
        step, end = ((1, ZS - 1), (-1, 0))[way]

        @pl.when(p.z != end)
        def _():
            remote(src, self.plane(zp).mine.at[self.s.all_a], self.zsems.under(way)[zp], p.column(p.z + step))

    def arrive(self, way, zp):
        mine = self.plane(zp).mine
        part = mine.at[self.s.all_a]
        wait_for(part, self.zsems.under(way)[zp][1])
        self.send_z(way, zp, part)
        self.spread(zp, mine)

    def relay(self, way, zp):
        self.plane(zp).relay()

    def finish(self, way, zp):
        def forward(block):
            part = block.at[self.s.all_a]
            self.forward(zp, part, part)

        self.plane(zp).rest(forward)

    def at_distance(self, d, *fns):
        z = self.p.z
        for fn in fns:
            if d:
                pl.when(z >= d)(functools.partial(fn, 0, z - d))
                pl.when(z + d < ZS)(functools.partial(fn, 1, z + d))
            else:
                fn(0, z)

    def band_out(self):
        p, band = self.p, self.band(self.p.z)
        self.forward(p.z, band, band)
        p.elsewhere(lambda zp: remote(band, band, (self.bsems[zp][0], self.bsems[p.z][1]), p.column(zp)))

    def band_in(self, zp):
        band = self.band(zp)
        wait_for(band, self.bsems[zp][1])
        self.forward(zp, band, band)

    def run(self, fill=lambda: None):
        p = self.p
        local(self.own, self.slab.mine, self.lsem)
        self.slab.start(self.own)
        for way in range(TWO):
            self.send_z(way, p.z, self.own.at[self.s.all_a])
        self.spread(p.z, self.own)
        fill()
        self.slab.relay()
        wait_for(self.own, self.lsem)
        near, mid, far = range(1, ZS)
        self.at_distance(0, self.relay)
        fill()
        self.at_distance(near, self.arrive)
        fill()
        self.at_distance(mid, self.arrive)
        self.slab.rest()
        self.band_out()
        self.at_distance(0, self.finish)
        fill()
        self.at_distance(near, self.relay)
        self.at_distance(far, self.arrive)
        fill()
        self.at_distance(near, self.finish)
        self.at_distance(mid, self.relay, self.finish)
        self.at_distance(far, self.relay)
        p.elsewhere(self.band_in)
        self.at_distance(far, self.finish)
        self.slab.drain()
        p.elsewhere(lambda zp: wait_for(self.band(zp), self.bsems[zp][0]))
        part = self.slab.mine.at[self.s.all_a]

        def sent(way, zp):
            wait_for(part, self.zsems.under(way)[zp][0])

        for zp in range(ZS):
            for sem in self.csems[zp]:
                wait_for(self.out.at[zp, :, :, p.c], sem)
            self.plane(zp).drain()
            for way, cond in enumerate(((p.z < ZS - 1) & (p.z >= zp), (p.z > 0) & (p.z <= zp))):
                pl.when(cond)(functools.partial(sent, way, zp))


class Filler:
    def __init__(self, body, share):
        self.body, self.share, self.at = body, share, 0

    def __call__(self):
        stop = min(self.at + self.share, TILES)
        if self.at < stop:
            lax.fori_loop(self.at, stop, lambda i, carry: self.body(i) or carry, 0)
        self.at = stop

    def finish(self):
        while self.at < TILES:
            self()


def tile_at(i):
    return pl.ds(pl.multiple_of(i * TILE, 128), TILE)


def drain_tiles(buf, sems):
    for slot in range(TWO):
        wait_for(buf.at[slot], sems.at[slot])


def comm_params(ident):
    return pltpu.CompilerParams(collective_id=ident, has_side_effects=True, vmem_limit_bytes=VMEM_LIMIT)


def gather_kernel(split, own, d_mods, act, out, wgrad, mods, acc, load_sem, tile_sem, *scratch):
    local(d_mods, mods, load_sem)
    peers = Peers()
    peers.barrier()

    def tile(i):
        slot = lax.rem(i, TWO)

        @pl.when(i >= TWO)
        def _():
            wait_for(acc.at[slot], tile_sem.at[slot])

        @pl.when(i == 0)
        def _():
            wait_for(mods, load_sem)

        acc[slot] = lax.dot_general(mods[:, tile_at(i)], act[...], CONTRACT_ROWS, preferred_element_type=F32)
        local(acc.at[slot], wgrad.at[tile_at(i)], tile_sem.at[slot])

    fill = Filler(tile, 3)
    AllGather(peers, own, out, split, scratch).run(fill)
    fill.finish()
    drain_tiles(acc, tile_sem)


def gather_blocks(block, d_mods, act):
    split = Split(*WMOD_SPLIT)
    return pl.pallas_call(
        functools.partial(gather_kernel, split),
        out_shape=[jax.ShapeDtypeStruct((ZS, TWO, TWO, TWO, split.rows, WIDTH), block.dtype), jax.ShapeDtypeStruct((MOD, WIDTH), F32)],
        in_specs=[ANY, ANY, IN_VMEM], out_specs=[ANY, ANY],
        scratch_shapes=[pltpu.VMEM(d_mods.shape, BF16), pltpu.VMEM((TWO, TILE, WIDTH), F32), DMA, DMA((TWO,)), *AllGather.scratch],
        compiler_params=comm_params(0), name="gather_wmod",
    )(block, d_mods, act)


def scatter_kernel(pieces, split, source, out, sem, *scratch):
    peers = Peers()
    peers.barrier()
    rs = ReduceScatter(peers, [source], pieces, split, scratch)
    rs.run()
    local(rs.part.at[peers.z, peers.y, peers.x], out, sem)
    rs.drain()
    wait_for(out, sem)


def scatter_sum(partial, pieces):
    split = Split(*WGRAD_SPLIT)
    return pl.pallas_call(
        functools.partial(scatter_kernel, pieces, split),
        out_shape=jax.ShapeDtypeStruct((split.rows, WIDTH), F32),
        in_specs=[ANY], out_specs=ANY, scratch_shapes=[DMA] + ReduceScatter.scratch(split),
        compiler_params=comm_params(1), name="scatter_wgrad",
    )(partial)


def reduce_kernel(pieces, split, count, *refs):
    sources, (act, weight, bias, out, mods, tiles, acc, load_sem, tile_sem), scratch = refs[:count], refs[count:count + 9], refs[count + 9:]
    peers = Peers()
    peers.barrier()

    def load(i):
        slot = lax.rem(i, TWO)
        local(weight.at[tile_at(i)], tiles.at[slot], load_sem.at[slot])

    def tile(i):
        slot = lax.rem(i, TWO)

        @pl.when(i >= TWO)
        def _():
            wait_for(acc.at[slot], tile_sem.at[slot])

        @pl.when(i < TILES - 1)
        def _():
            load(i + 1)

        wait_for(tiles.at[slot], load_sem.at[slot])
        product = lax.dot_general(act[...], tiles[slot], CONTRACT_COLS, preferred_element_type=F32)
        acc[slot] = (product + bias[:, tile_at(i)]).astype(BF16)
        local(acc.at[slot], mods.at[:, tile_at(i)], tile_sem.at[slot])

    load(0)
    fill = Filler(tile, 3)
    own = len(AllGather.scratch)
    rs = ReduceScatter(peers, sources, pieces, split, scratch[own:])
    rs.run(fill)
    fill.finish()
    AllGather(peers, rs.part.at[peers.z, peers.y, peers.x], out, split, scratch[:own]).run()
    rs.drain()
    drain_tiles(acc, tile_sem)


def reduce_all(sources, pieces, act, weight, bias):
    split = Split(*EMBED_SPLIT)
    return pl.pallas_call(
        functools.partial(reduce_kernel, pieces, split, len(sources)),
        out_shape=[jax.ShapeDtypeStruct((ZS, TWO, TWO, TWO, split.rows, WIDTH), F32), jax.ShapeDtypeStruct((ROWS, MOD), BF16)],
        in_specs=[ANY] * len(sources) + [IN_VMEM, ANY, IN_VMEM], out_specs=[ANY, ANY],
        scratch_shapes=[pltpu.VMEM((TWO, TILE, WIDTH), BF16), pltpu.VMEM((TWO, ROWS, TILE), BF16), DMA((TWO,)), DMA((TWO,)), *AllGather.scratch] + ReduceScatter.scratch(split),
        compiler_params=comm_params(TWO), name="reduce_embed",
    )(*sources, act, weight, bias)


def unpack_kernel(pieces, total, *refs):
    *outs, buf, load_sem, store_sem = refs
    order = [(zp, core) for zp in range(ZS) for core in range(TWO)]
    for at in order:
        local(total.at[at[0], :, :, at[1]], buf.at[at], load_sem.at[at])
    for at in order:
        wait_for(buf.at[at], load_sem.at[at])
        zp, core = at
        for dst, start, n, row in pieces[core]:
            local(buf.at[zp, core, :, :, pl.ds(row, n)], outs[dst].at[zp, :, :, pl.ds(start, n)], store_sem.at[at])
    for at in order:
        wait_for(buf.at[at], store_sem.at[at])


def unpack(total, sources, pieces):
    return pl.pallas_call(
        functools.partial(unpack_kernel, pieces),
        out_shape=[jax.ShapeDtypeStruct(s.shape, s.dtype) for s in sources],
        in_specs=[ANY], out_specs=[ANY] * len(sources),
        scratch_shapes=[pltpu.VMEM((ZS, TWO, TWO, TWO, *total.shape[ZS:]), F32), DMA((ZS, TWO)), DMA((ZS, TWO))],
        compiler_params=pltpu.CompilerParams(vmem_limit_bytes=VMEM_LIMIT), name="unpack",
    )(total)


def outer_kernel(left, right, out):
    out[...] = lax.dot_general(left[...], right[...], CONTRACT_ROWS, preferred_element_type=F32)


def outer(left, right):
    rows, n = left.shape
    return pl.pallas_call(
        outer_kernel,
        grid=(n // rows,),
        out_shape=jax.ShapeDtypeStruct((n, WIDTH), F32),
        in_specs=[pl.BlockSpec((rows, rows), lambda i: (0, i)), pl.BlockSpec((rows, WIDTH), lambda i: (0, 0))],
        out_specs=pl.BlockSpec((rows, WIDTH), lambda i: (i, 0)),
        compiler_params=pltpu.CompilerParams(vmem_limit_bytes=VMEM_LIMIT), name="outer",
    )(left, right)


def sinusoid(values, freq_width):
    half_width = freq_width // 2
    freq_table = jnp.exp(-math.log(MAX_PERIOD) * jnp.arange(half_width, dtype=F32) / half_width)
    angles = (TIME_SCALE * values)[:, None] * freq_table[None, :]
    return jnp.concatenate([jnp.cos(angles), jnp.sin(angles)], axis=1).astype(BF16)


def silu_grad(values):
    sigmoid_v = jax.nn.sigmoid(values)
    return sigmoid_v * (1.0 + values * (1.0 - sigmoid_v))


def mlp_forward(inputs_bf, params):
    hidden = jnp.dot(inputs_bf, params[0], preferred_element_type=F32) + params[1].astype(F32)
    act_bf = jax.nn.silu(hidden).astype(BF16)
    output = jnp.dot(act_bf, params[2], preferred_element_type=F32) + params[3].astype(F32)
    return output, hidden, act_bf


def mlp_backward(inputs_bf, params, hidden, act_bf, d_out_bf):
    grad_w2 = lax.dot_general(act_bf, d_out_bf, CONTRACT_ROWS, preferred_element_type=F32)
    d_act = lax.dot_general(d_out_bf, params[2], CONTRACT_COLS, preferred_element_type=F32)
    d_hidden = d_act * silu_grad(hidden)
    d_hidden_bf = d_hidden.astype(BF16)
    if inputs_bf.shape[1] > d_hidden_bf.shape[1]:
        grad_w1 = outer(inputs_bf, d_hidden_bf)
    else:
        grad_w1 = lax.dot_general(inputs_bf, d_hidden_bf, CONTRACT_ROWS, preferred_element_type=F32)
    grad_b1 = jnp.sum(d_hidden, axis=0)
    return grad_w1, grad_b1, grad_w2


def by_chip(grad):
    return grad.reshape(ZS, TWO, TWO, grad.shape[0] // CHIPS, WIDTH)


WGRAD_PIECES = (((0, 0, 184, 0),), ((0, 176, 184, 0),))
EMBED_PIECES = (
    ((0, 0, 16, 0), (1, 0, 16, 16), (2, 0, 128, 32), (6, 0, 8, 160), (3, 0, 24, 168)),
    ((3, 24, 48, 0), (4, 0, 72, 48), (5, 0, 72, 120)),
)


def solution(mesh):
    row_split = P(AXIS)
    row_matrix = P(AXIS, None)
    col_matrix = P(None, AXIS)
    embed_specs = (P(None, None), P(None), P(None, None), P(None)) * 3
    in_specs = (row_split, row_split, row_matrix) + embed_specs + (col_matrix, row_split, row_matrix)
    out_specs = (row_matrix, col_matrix, row_split) + embed_specs

    def local_step(timesteps, guidance, pooled, time_w1, time_b1, time_w2, time_b2, guide_w1, guide_b1, guide_w2, guide_b2, text_w1, text_b1, text_w2, text_b2, w_mod, b_mod, d_mods):
        me = lax.axis_index(AXIS)
        freq_width = time_w1.shape[0]
        inputs_list = [sinusoid(timesteps, freq_width), sinusoid(guidance, freq_width), pooled]
        params_list = [(time_w1, time_b1, time_w2, time_b2), (guide_w1, guide_b1, guide_w2, guide_b2), (text_w1, text_b1, text_w2, text_b2)]
        saved = [mlp_forward(u, params) for u, params in zip(inputs_list, params_list)]
        cond_vec = saved[0][0] + saved[1][0] + saved[2][0]
        cond_silu = jax.nn.silu(cond_vec).astype(BF16)

        extra = jnp.pad(b_mod[None, :], ((0, PADDED - SHARE - 1), (0, WIDTH - SHARE)))
        gathered, part_wgrad = gather_blocks(jnp.concatenate([w_mod.T, extra], axis=0), d_mods, cond_silu)
        gathered = gathered.reshape(DEVICES, PADDED, WIDTH)
        full_wt = gathered[:, :SHARE].reshape(MOD, WIDTH)
        full_b = gathered[:, SHARE, :SHARE].reshape(1, MOD).astype(F32)
        wgrad = scatter_sum(by_chip(part_wgrad), WGRAD_PIECES)
        grad_wmod = lax.dynamic_slice(wgrad, (4 * lax.rem(me, TWO), 0), (SHARE, WIDTH)).T

        d_cond = jnp.dot(d_mods, full_wt, preferred_element_type=F32)
        d_vec = d_cond * silu_grad(cond_vec)
        d_vec_bf = d_vec.astype(BF16)
        grads = [mlp_backward(u, params, record[1], record[2], d_vec_bf) for u, params, record in zip(inputs_list, params_list, saved)]
        bgrad_rows = MOD // WIDTH
        part_bgrad = jnp.sum(d_mods, axis=0, dtype=F32).reshape(bgrad_rows, WIDTH)
        vectors = [g[1] for g in grads] + [jnp.sum(d_vec, axis=0)]
        vectors = jnp.concatenate([jnp.stack(vectors), part_bgrad], axis=0)
        vectors = jnp.pad(vectors, ((0, 128 - vectors.shape[0]), (0, 0)))
        sources = [by_chip(g) for g in [g[0] for g in grads] + [g[2] for g in grads] + [vectors]]
        total, modulation = reduce_all(sources, EMBED_PIECES, cond_silu, full_wt, full_b)
        *full, sums = [g.reshape(-1, WIDTH) for g in unpack(total, sources, EMBED_PIECES)]
        count = len(grads)
        grad_bmod = lax.dynamic_slice(sums[ZS:ZS + bgrad_rows].reshape(MOD), (SHARE * me,), (SHARE,))
        embed_grads = [g for i in range(count) for g in (full[i], sums[i], full[i + count], sums[count])]
        return (modulation, grad_wmod, grad_bmod, *embed_grads)

    return jax.shard_map(local_step, mesh=mesh, in_specs=in_specs, out_specs=out_specs, check_vma=False)
```

time: 814 us -> 577 us (0.71)
  blocking collectives: 486 us -> 0 us
  Pallas kernels: 0 us -> 467 us
  waiting for transfers between devices: 127 us -> 0 us
  matrix products: 95.1 us -> 52.3 us
  local copies, waits for them, and re-layouts: 59.5 us -> 34.3 us
  starting transfers between devices: 17.7 us -> 0 us
  between operations: 14.8 us -> 1.38 us
    unnamed x3 -> x0, blocking collectives: 486 us -> none
    pallas_call x0 -> x5, Pallas kernels: none -> 467 us  [the longest x1 241 us: reduce_all(): pl.pallas_call(functools.partial(reduce_kernel, pieces, split, len(source...]
    all_gather x1 -> x0, waiting for transfers between devices: 83 us -> none  [local_step(): full_wmod = lax.all_gather(w_mod, MESH_AXIS, axis=1, tiled=True)]
    unnamed x67 -> x51, local copies, waits for them, and re-layouts: 59.5 us -> 9.88 us
    dot_general x15 -> x12, matrix products: 89.2 us -> 44.3 us  [the longest x1 14 us: local_step(): d_cond = jnp.dot(d_mods, full_wt, preferred_element_type=F32)]
    psum x1 -> x0, waiting for transfers between devices: 42.8 us -> none  [local_step(): lax.psum(embed_backward(inputs_list, params_list, saved_acts, d_vec), MES...]
    unnamed x2 -> x0, starting transfers between devices: 17.6 us -> none
    reshape x0 -> x3, local copies, waits for them, and re-layouts: none -> 16.4 us  [the longest x1 16.4 us: local_step(): full_wt = gathered[:, :SHARE].reshape(MOD, WIDTH)]
  transfers between devices with their start and end apart: 4 -> 0, of which waited for: 2 -> 0; matrix products, arithmetic and copies ran while one was open for 53% -> 0% of each run, Pallas kernels for 0% -> 0%
where the time goes in v1:
time: 577 us; the launch traced here: 567 us
  Pallas kernels  467 us (81%)
  matrix products  52.3 us (9%)
  local copies, waits for them, and re-layouts  34.3 us (6%)
  other arithmetic  12.9 us (2%)
    pallas_call x1, Pallas kernels, reduce_all(): pl.pallas_call(functools.partial(reduce_kernel, pieces, split, len(source...  241 us
    pallas_call x1, Pallas kernels, scatter_sum(): pl.pallas_call(functools.partial(scatter_kernel, pieces, split), out_shap...  123 us
    pallas_call x1, Pallas kernels, gather_blocks(): pl.pallas_call(functools.partial(gather_kernel, split), out_shape=[jax.Sh...  76.9 us
    pallas_call x1, Pallas kernels, unpack(): pl.pallas_call(functools.partial(unpack_kernel, pieces), out_shape=[jax.S...  18.6 us
    reshape x1, local copies, waits for them, and re-layouts, local_step(): full_wt = gathered[:, :SHARE].reshape(MOD, WIDTH)  16.4 us
    dot_general x1, matrix products, local_step(): d_cond = jnp.dot(d_mods, full_wt, preferred_element_type=F32)  14 us
    dot_general x3, matrix products, mlp_backward(): lax.dot_general(act_bf, d_out_bf, CONTRACT_ROWS, preferred_element_type=F32)  13.9 us

profile of v1, /device:TPU:0, one launch (start us, length us, event | category | flops | bytes accessed | tf_op | source)
XLA Modules:
  0.0 567.4 jit_solution(14579897774251841055)
XLA Ops:
  0.6 0.0 copy-start
  0.7 0.7 broadcast_in_dim.2
  1.4 0.7 broadcast_multiply_fusion
  2.1 0.7 convert_element_type.56
  2.8 0.7 convert_element_type.58
  3.5 0.7 convert_element_type.59
  4.2 0.7 convert_element_type.61
  4.9 0.7 convert_element_type.62
  5.5 0.7 convert_element_type.64
  6.2 4.0 convert_reduce_fusion
  10.3 0.8 fusion.8.own
  11.1 2.2 fusion.11
  13.3 0.5 convolution_add_fusion
  13.9 0.5 convolution_add_fusion.1
  14.4 1.9 copy-done.7
  16.3 2.9 convolution_add_fusion.3
  19.2 2.1 convolution_add_fusion.5
  21.3 0.5 copy-done.14
  21.8 2.1 fusion.1
  24.0 3.9 multiply_convert_fusion
  27.9 76.9 %gather_wmod.1 = (bf16[4,2,2,2,184,1152]{5,4,3,2,1,0:T(8,128)(2,1)}, f32[5760,1152]{1,0:T(8,128)}) custom-call(bf16[184,1152]{1,0:T(8,128)(2,1)} %fusion.8.own, bf16[512,5760]{1,0:T(8,128)(2,1)} %d_mods.1, bf16[512,1152]{1,0:T(8,128)(2,1)} %get-tuple-element.51.act.refs_7_), custom_call_target="tpu_custom_call" | custom-call | tf_op jit(solution)/shard_map/gather_wmod/pallas_call | solution.py:507
  104.8 123.1 %scatter_wgrad.1 = f32[184,1152]{1,0:T(8,128)} custom-call(f32[4,2,2,360,1152]{4,3,2,1,0:T(8,128)} %bitcast.45), custom_call_target="tpu_custom_call" | custom-call | tf_op jit(solution)/shard_map/scatter_wgrad/pallas_call | solution.py:528
  227.9 2.1 dynamic-slice_bitcast_fusion
  230.0 1.0 fusion.13
  231.0 0.8 reshape.133.refs_9_
  231.8 16.4 %reshape.115.refs_8_ = bf16[5760,1152]{1,0:T(8,128)(2,1)} reshape(bf16[32,180,1152]{2,1,0:T(8,128)(2,1)} %bitcast.47) | data formatting | bytes 26542080 | tf_op jit(solution)/shard_map/reshape | solution.py:686
  248.2 14.0 %fusion.21 = (f32[1152]{0:T(1024)S(1)}, bf16[512,1152]{1,0:T(8,128)(2,1)S(1)}) fusion(f32[512,1152]{1,0:T(8,128)S(1)} %copy-done.23, bf16[512,5760]{1,0:T(8,128)(2,1)} %d_mods.1, bf16[5760,1152]{1,0:T(8,128)(2,1)} %reshape.115.refs_8_), kind=kOutput, calls=%fused_computation.56 | convolution fusion | flops 6800669696 | bytes 22712832 | tf_op jit(solution)/shard_map/dot_general | solution.py:691
  262.3 0.0 copy-start.15
  262.3 3.0 fusion.22
  265.3 2.0 fusion.24
  267.4 1.5 fusion.3
  268.9 0.5 copy-done.5
  269.4 3.0 fusion.23
  272.3 0.3 concatenate.17
  272.7 0.9 pad.9
  273.6 2.9 fusion.5
  276.4 5.6 fusion.18
  282.0 4.2 fusion.19
  286.2 4.2 fusion.20
  290.4 7.5 %outer.1 = f32[2048,1152]{1,0:T(8,128)} custom-call(bf16[512,2048]{1,0:T(8,128)(2,1)} %left.1, bf16[512,1152]{1,0:T(8,128)(2,1)} %get-tuple-element.44.right), custom_call_target="tpu_custom_call" | custom-call | tf_op jit(solution)/shard_map/outer/pallas_call | solution.py:613
  297.8 240.6 %reduce_embed.1 = (f32[4,2,2,2,192,1152]{5,4,3,2,1,0:T(8,128)}, bf16[512,5760]{1,0:T(8,128)(2,1)}) custom-call(f32[4,2,2,16,1152]{4,3,2,1,0:T(8,128)} %bitcast.52, f32[4,2,2,16,1152]{4,3,2,1,0:T(8,128)} %bitcast.51, f32[4,2,2,128,1152]{4,3,2,1,0:T(8,128)} %bitcast.44, f32[4,2,2,72,1152]{4,3,2,1,0:T(8,128)} %bitcast.48, f32[4,2,2,72,1152]{4,3,2,1,0:T(8,128)} %bitcast.49, ...), custom_call_target="tpu_custom_call" | custom-call | tf_op jit(solution)/shard_map/reduce_embed/pallas_call | solution.py:574
  538.4 18.6 %unpack.1 = (f32[4,2,2,16,1152]{4,3,2,1,0:T(8,128)}, f32[4,2,2,16,1152]{4,3,2,1,0:T(8,128)}, f32[4,2,2,128,1152]{4,3,2,1,0:T(8,128)}, f32[4,2,2,72,1152]{4,3,2,1...) custom-call(f32[4,2,2,2,192,1152]{5,4,3,2,1,0:T(8,128)} %get-tuple-elemen, ...), custom_call_target="tpu_custom_call" | custom-call | tf_op jit(solution)/shard_map/unpack/pallas_call | solution.py:598
  557.0 1.6 slice_reduce_fusion
  558.6 0.9 slice.32
  559.5 0.6 dynamic_slice.7
  560.2 0.6 copy.37
  560.8 0.6 copy.38
  561.4 5.7 %copy.39 = bf16[512,5760]{1,0:T(8,128)(2,1)} copy(bf16[512,5760]{1,0:T(8,128)(2,1)} %get-tuple-element.110) | data formatting | bytes 11796480
  (50 shorter events, 0.1 us)
Async XLA Ops:
  0.6 12.7 %copy-start = (bf16[256,1152]{1,0:T(8,128)(2,1)S(1)}, bf16[256,1152]{1,0:T(8,128)(2,1)}, u32[]{:S(2)}) copy-start(bf16[256,1152]{1,0:T(8,128)(2,1)} %param.25) | copy-start | bytes 1769476
  6.2 4.0 copy-start.9
  10.3 3.6 copy-start.8
  11.1 3.3 copy-start.11
  13.8 7.5 %copy-start.2 = (f32[512,1152]{1,0:T(8,128)}, f32[512,1152]{1,0:T(8,128)S(1)}, u32[]{:S(2)}) copy-start(f32[512,1152]{1,0:T(8,128)S(1)} %convolution_add_fusion) | copy-start | bytes 7077892
  13.8 2.4 copy-start.7
  16.3 2.9 copy-start.4
  16.3 2.9 copy-start.16
  19.2 4.7 copy-start.18
  19.2 2.6 copy-start.14
  21.8 2.1 copy-start.12
  231.8 16.4 %copy-start.23 = (f32[512,1152]{1,0:T(8,128)S(1)}, f32[512,1152]{1,0:T(8,128)}, u32[]{:S(2)}) copy-start(f32[512,1152]{1,0:T(8,128)} %get-tuple-element.52) | copy-start | bytes 7077892
  248.2 14.0 %copy-start.13 = (bf16[1152,1152]{1,0:T(8,128)(2,1)S(1)}, bf16[1152,1152]{1,0:T(8,128)(2,1)}, u32[]{:S(2)}) copy-start(bf16[1152,1152]{1,0:T(8,128)(2,1)} %param.31) | copy-start | bytes 7962628
  248.2 14.0 %copy-start.19 = (f32[512,1152]{1,0:T(8,128)S(1)}, f32[512,1152]{1,0:T(8,128)}, u32[]{:S(2)}) copy-start(f32[512,1152]{1,0:T(8,128)} %copy-done.18) | copy-start | bytes 7077892
  262.2 6.7 %copy-start.21 = (bf16[512,1152]{1,0:T(8,128)(2,1)}, bf16[512,1152]{1,0:T(8,128)(2,1)S(1)}, u32[]{:S(2)}) copy-start(bf16[512,1152]{1,0:T(8,128)(2,1)S(1)} %get-tuple-element.42) | copy-start | bytes 3538948
  262.3 3.1 copy-start.3
  262.3 3.1 copy-start.15
  265.3 3.6 copy-start.17
  267.3 2.0 copy-start.5
  272.7 3.7 copy-start.6
  276.4 5.6 copy-start.22
  282.0 4.2 copy-start.20
  558.6 8.5 %copy-start.10 = (f32[1152]{0:T(1024)}, f32[1152]{0:T(1024)S(1)}, u32[]{:S(2)}) copy-start(f32[1152]{0:T(1024)S(1)} %get-tuple-element.116) | copy-start | bytes 13828
  561.4 5.7 %copy-start.1 = (bf16[256,1152]{1,0:T(8,128)(2,1)S(1)}, bf16[256,1152]{1,0:T(8,128)(2,1)}, u32[]{:S(2)}) copy-start(bf16[256,1152]{1,0:T(8,128)(2,1)} %param.25) | copy-start | bytes 1769476

commit v2 on v1

--- a/solution.py
+++ b/solution.py
@@ -168,7 +168,7 @@
 class ReduceScatter:
     @staticmethod
     def scratch(s):
-        whole = [(ZS, TWO, TWO, s.rows)] * TWO
+        whole = [(n, TWO, TWO, s.rows) for n in (ZS, TWO)]
         planes = [(ZS,) + shape for shape in PlaneReduce.shapes(s.n[0])] + PlaneReduce.shapes(s.n[1])
         shapes = whole + planes + [(TWO, ZS, s.a), (ZS, TWO, TWO, s.b)]
         buffers = [pltpu.VMEM(shape + (WIDTH,), F32) for shape in shapes]
@@ -178,30 +178,38 @@
         self.p, self.sources, self.pieces, self.s = p, sources, pieces, s
         scratch = list(scratch)
         take = lambda n: [scratch.pop(0) for _ in range(n)]
-        self.part, self.fromc = take(TWO)
+        self.part, self.own = take(TWO)
         boxes, slab_boxes = take(ZS), take(ZS)
         self.line, self.slabs, self.lsem = take(3)
         self.csems, plane_sems, self.zsems, self.bsems, slab_sems = (Sems(take(TWO)) for _ in range(5))
         self.planes = [PlaneReduce(p, self.part.at[zp], s.colours[0], [box.at[zp] for box in boxes], plane_sems.under(zp)) for zp in range(ZS)]
         self.slab = PlaneReduce(p, self.part.at[p.z], s.colours[1], slab_boxes, slab_sems)
 
-    def begin(self, zp):
-        p = self.p
-
-        def load(core):
-            mine = self.pieces[core]
+    def partner(self, zp):
+        def send(core):
             for src, start, n, at in self.pieces[1 - core]:
-                remote(self.sources[src].at[zp, :, :, pl.ds(start, n)], self.fromc.at[zp, :, :, pl.ds(at, n)], self.csems[zp], p.core)
-            for src, start, n, at in mine:
-                local(self.sources[src].at[zp, :, :, pl.ds(start, n)], self.part.at[zp, :, :, pl.ds(at, n)], self.lsem.at[zp])
-
+                remote(self.sources[src].at[zp, :, :, pl.ds(start, n)], self.part.at[zp, :, :, pl.ds(at, n)], self.csems[zp], self.p.core)
+
+        self.by_core(send)
+
+    def load(self, zp):
+        slot = Z_ORDER.index(zp) % TWO
+
+        def start(core):
+            for src, at_src, n, at in self.pieces[core]:
+                local(self.sources[src].at[zp, :, :, pl.ds(at_src, n)], self.own.at[slot, :, :, pl.ds(at, n)], self.lsem.at[zp])
+
+        self.by_core(start)
+
+    def by_core(self, fn):
         for core in range(TWO):
-            pl.when(p.c == core)(functools.partial(load, core))
+            pl.when(self.p.c == core)(functools.partial(fn, core))
 
     def both_cores(self, zp):
-        wait_for(self.part.at[zp], self.lsem.at[zp])
-        wait_for(self.fromc.at[zp], self.csems[zp][1])
-        add_rows(self.part.at[zp], self.fromc.at[zp])
+        own = self.own.at[Z_ORDER.index(zp) % TWO]
+        wait_for(own, self.lsem.at[zp])
+        wait_for(self.part.at[zp], self.csems[zp][1])
+        add_rows(self.part.at[zp], own)
 
     def slab_out(self, zp):
         p = self.p
@@ -252,7 +260,7 @@
                 wait_for(self.line.at[way, zp, part], self.zsems.under(way).under(zp)[k][0])
 
         for zp in range(ZS):
-            wait_for(self.fromc.at[zp], self.csems[zp][0])
+            wait_for(self.part.at[zp], self.csems[zp][0])
             self.planes[zp].drain()
             for way, cond in enumerate((p.z < zp, p.z > zp)):
                 pl.when(cond)(functools.partial(sent, way, zp))
@@ -261,13 +269,19 @@
         one, two, three, four = Z_ORDER
         planes = self.planes
         for zp in Z_ORDER:
-            self.begin(zp)
-        for zp in Z_ORDER:
+            self.partner(zp)
+        self.load(one)
+        self.load(two)
+        fill()
+        for zp, later in zip(Z_ORDER, (three, four, None, None)):
             self.both_cores(zp)
-            if zp in (one, two):
+            if later is None:
+                self.slab_out(zp)
+            else:
+                self.load(later)
                 planes[zp].start()
-            self.slab_out(zp)
-        fill()
+                self.slab_out(zp)
+            fill()
         planes[one].middle()
         planes[three].start()
         fill()
@@ -290,14 +304,17 @@
         fill()
         self.p.elsewhere(self.slab_sum)
         self.slab.start()
+        fill()
         planes[four].middle()
         self.slab.middle()
+        fill()
         planes[four].end()
         self.hop(four, 0)
         self.hop(three, 1)
         self.hop(two, TWO)
         self.hop(four, 1)
         self.slab.end()
+        fill()
         for zp in Z_ORDER:
             self.final(zp)
 
@@ -449,57 +466,122 @@
                 pl.when(cond)(functools.partial(sent, way, zp))
 
 
+class Job:
+    def __init__(self, count, body, load=None):
+        self.count, self.body, self.load = count, body, load
+
+
 class Filler:
-    def __init__(self, body, share):
-        self.body, self.share, self.at = body, share, 0
+    def __init__(self, jobs, share):
+        self.jobs, self.share, self.job, self.at = jobs, share, 0, 0
+
+    def prime(self):
+        self.jobs[0].load(0)
+
+    def part(self, stop):
+        job, last = self.jobs[self.job], self.jobs[self.job].count - 1
+        after = next((j.load for j in self.jobs[self.job + 1:] if j.load), None)
+
+        def tile(i, carry):
+            if job.load:
+                @pl.when(i < last)
+                def _():
+                    job.load(i + 1)
+
+                if after:
+                    pl.when(i == last)(lambda: after(0))
+            job.body(i)
+            return carry
+
+        lax.fori_loop(self.at, stop, tile, 0)
 
     def __call__(self):
-        stop = min(self.at + self.share, TILES)
-        if self.at < stop:
-            lax.fori_loop(self.at, stop, lambda i, carry: self.body(i) or carry, 0)
-        self.at = stop
+        left = self.share
+        while left and self.job < len(self.jobs):
+            count = self.jobs[self.job].count
+            stop = min(self.at + left, count)
+            self.part(stop)
+            left -= stop - self.at
+            self.at = stop
+            if stop == count:
+                self.job, self.at = self.job + 1, 0
 
     def finish(self):
-        while self.at < TILES:
+        while self.job < len(self.jobs):
             self()
 
 
-def tile_at(i):
-    return pl.ds(pl.multiple_of(i * TILE, 128), TILE)
-
-
-def drain_tiles(buf, sems):
-    for slot in range(TWO):
-        wait_for(buf.at[slot], sems.at[slot])
+class Stream:
+    def __init__(self, buf, sems, base=0):
+        self.buf, self.sems, self.base = buf, sems, base
+
+    def slot(self, i):
+        return lax.rem(i + self.base, TWO)
+
+    def load(self, i, src):
+        slot = self.slot(i)
+        local(src, self.buf.at[slot], self.sems.at[slot])
+
+    def ready(self, i):
+        slot = self.slot(i)
+        wait_for(self.buf.at[slot], self.sems.at[slot])
+        return self.buf[slot]
+
+    def store(self, i, value, dst):
+        slot = self.slot(i)
+
+        @pl.when(i + self.base >= TWO)
+        def _():
+            wait_for(self.buf.at[slot], self.sems.at[slot])
+
+        self.buf[slot] = value
+        local(self.buf.at[slot], dst, self.sems.at[slot])
+
+    def drain(self):
+        for slot in range(TWO):
+            wait_for(self.buf.at[slot], self.sems.at[slot])
+
+    def after(self, count):
+        return Stream(self.buf, self.sems, self.base + count)
+
+    @staticmethod
+    def scratch(dtype, *shape):
+        return [pltpu.VMEM((TWO, *shape), dtype), DMA((TWO,))]
+
+
+def tile_at(i, width=TILE, start=0):
+    return pl.ds(pl.multiple_of(start + i * width, 128), width)
+
+
+def dot_rows(left, right):
+    return lax.dot_general(left, right, CONTRACT_ROWS, preferred_element_type=F32)
+
+
+def dot_cols(left, right):
+    return lax.dot_general(left, right, CONTRACT_COLS, preferred_element_type=F32)
 
 
 def comm_params(ident):
     return pltpu.CompilerParams(collective_id=ident, has_side_effects=True, vmem_limit_bytes=VMEM_LIMIT)
 
 
-def gather_kernel(split, own, d_mods, act, out, wgrad, mods, acc, load_sem, tile_sem, *scratch):
+def gather_kernel(split, own, d_mods, act, out, wgrad, mods, load_sem, *scratch):
     local(d_mods, mods, load_sem)
     peers = Peers()
     peers.barrier()
+    tiles, scratch = Stream(*scratch[:TWO]), scratch[TWO:]
 
     def tile(i):
-        slot = lax.rem(i, TWO)
-
-        @pl.when(i >= TWO)
-        def _():
-            wait_for(acc.at[slot], tile_sem.at[slot])
-
         @pl.when(i == 0)
         def _():
             wait_for(mods, load_sem)
 
-        acc[slot] = lax.dot_general(mods[:, tile_at(i)], act[...], CONTRACT_ROWS, preferred_element_type=F32)
-        local(acc.at[slot], wgrad.at[tile_at(i)], tile_sem.at[slot])
-
-    fill = Filler(tile, 3)
+        tiles.store(i, dot_rows(mods[:, tile_at(i)], act[...]), wgrad.at[tile_at(i)])
+
+    fill = Filler([Job(TILES, tile)], TWO)
     AllGather(peers, own, out, split, scratch).run(fill)
     fill.finish()
-    drain_tiles(acc, tile_sem)
+    tiles.drain()
 
 
 def gather_blocks(block, d_mods, act):
@@ -508,65 +590,129 @@
         functools.partial(gather_kernel, split),
         out_shape=[jax.ShapeDtypeStruct((ZS, TWO, TWO, TWO, split.rows, WIDTH), block.dtype), jax.ShapeDtypeStruct((MOD, WIDTH), F32)],
         in_specs=[ANY, ANY, IN_VMEM], out_specs=[ANY, ANY],
-        scratch_shapes=[pltpu.VMEM(d_mods.shape, BF16), pltpu.VMEM((TWO, TILE, WIDTH), F32), DMA, DMA((TWO,)), *AllGather.scratch],
+        scratch_shapes=[pltpu.VMEM(d_mods.shape, BF16), DMA, *Stream.scratch(F32, TILE, WIDTH), *AllGather.scratch],
         compiler_params=comm_params(0), name="gather_wmod",
     )(block, d_mods, act)
 
 
-def scatter_kernel(pieces, split, source, out, sem, *scratch):
+def scatter_kernel(pieces, split, mlps, *refs):
+    refs = list(refs)
+    take = lambda n: [refs.pop(0) for _ in range(n)]
+    source, d_mods, weight, cond = take(ZS)
+    hidden, second, inputs, acts = (take(mlps) for _ in range(ZS))
+    out, sums = take(TWO)
+    grads1, grads2 = take(mlps), take(mlps)
+    mods, dcond, cvec, sem, mods_sem, cond_sem = take(6)
+    wtiles, htiles, ltiles, stiles, lsmall, ssmall = (Stream(*take(TWO)) for _ in range(6))
+    small = lsmall.buf.shape[-1]
+    local(d_mods, mods, mods_sem)
+    local(cond, cvec, cond_sem)
     peers = Peers()
     peers.barrier()
-    rs = ReduceScatter(peers, [source], pieces, split, scratch)
-    rs.run()
+    rs = ReduceScatter(peers, [source], pieces, split, refs)
+
+    def vector(k):
+        return mods.at[:, pl.ds(k * WIDTH, WIDTH)]
+
+    def d_cond(i):
+        @pl.when(i == 0)
+        def _():
+            wait_for(mods, mods_sem)
+
+        product = jnp.dot(mods[:, tile_at(i)], wtiles.ready(i), preferred_element_type=F32)
+        dcond[...] = jnp.where(i == 0, 0.0, dcond[...]) + product
+
+    def d_vec(i):
+        @pl.when(i == 0)
+        def _():
+            wait_for(cvec, cond_sem)
+            sums[...] = jnp.zeros_like(sums)
+
+        at = tile_at(i, small)
+        value = dcond[at, :] * silu_grad(cvec[at, :])
+        mods[at, :WIDTH] = value.astype(BF16)
+        sums[mlps:mlps + 1, :] += jnp.sum(value, axis=0, keepdims=True)
+
+    per = WIDTH // TILE
+    jobs = [Job(TILES, d_cond, lambda i: wtiles.load(i, weight.at[tile_at(i)])), Job(ROWS // small, d_vec)]
+    for k in range(mlps):
+        w, h = wtiles.after(TILES + k * per), htiles.after(k * per)
+
+        def load(i, k=k, w=w, h=h):
+            w.load(i, second[k].at[tile_at(i)])
+            h.load(i, hidden[k].at[:, tile_at(i)])
+
+        def d_hidden(i, k=k, w=w, h=h):
+            value = dot_cols(vector(0)[...], w.ready(i)) * silu_grad(h.ready(i))
+            mods[:, tile_at(i, start=(k + 1) * WIDTH)] = value.astype(BF16)
+            sums[k:k + 1, tile_at(i)] = jnp.sum(value, axis=0, keepdims=True)
+
+        jobs.append(Job(per, d_hidden, load))
+
+    def outer(count, left, right, dst, lefts, stages, width):
+        def load(i):
+            lefts.load(i, left.at[:, tile_at(i, width)])
+
+        def body(i):
+            stages.store(i, dot_rows(lefts.ready(i), right[...]), dst.at[tile_at(i, width)])
+
+        jobs.append(Job(count, body, load))
+
+    done = 0
+    for k in range(mlps):
+        outer(per, acts[k], vector(0), grads2[k], ltiles.after(k * per), stiles.after(k * per), TILE)
+    for k in range(mlps):
+        count = inputs[k].shape[1] // small
+        outer(count, inputs[k], vector(k + 1), grads1[k], lsmall.after(done), ssmall.after(done), small)
+        done += count
+    fill = Filler(jobs, ZS)
+    fill.prime()
+    rs.run(fill)
     local(rs.part.at[peers.z, peers.y, peers.x], out, sem)
+    fill.finish()
+    stiles.drain()
+    ssmall.drain()
     rs.drain()
     wait_for(out, sem)
 
 
-def scatter_sum(partial, pieces):
+def scatter_sum(partial, d_mods, weight, cond, hidden, second, inputs, acts, pieces):
     split = Split(*WGRAD_SPLIT)
+    args = [partial, d_mods, weight, cond, *hidden, *second, *inputs, *acts]
+    small = inputs[0].shape[1]
+    grads = [jax.ShapeDtypeStruct((a.shape[1], WIDTH), F32) for a in (*inputs, *acts)]
     return pl.pallas_call(
-        functools.partial(scatter_kernel, pieces, split),
-        out_shape=jax.ShapeDtypeStruct((split.rows, WIDTH), F32),
-        in_specs=[ANY], out_specs=ANY, scratch_shapes=[DMA] + ReduceScatter.scratch(split),
+        functools.partial(scatter_kernel, pieces, split, len(hidden)),
+        out_shape=[jax.ShapeDtypeStruct((split.rows, WIDTH), F32), jax.ShapeDtypeStruct((8, WIDTH), F32), *grads],
+        in_specs=[ANY] * len(args), out_specs=[ANY, IN_VMEM] + [ANY] * len(grads),
+        scratch_shapes=[
+            pltpu.VMEM(d_mods.shape, BF16), pltpu.VMEM(cond.shape, F32), pltpu.VMEM(cond.shape, F32), DMA, DMA, DMA,
+            *Stream.scratch(BF16, TILE, WIDTH), *Stream.scratch(F32, ROWS, TILE), *Stream.scratch(BF16, ROWS, TILE), *Stream.scratch(F32, TILE, WIDTH),
+            *Stream.scratch(BF16, ROWS, small), *Stream.scratch(F32, small, WIDTH), *ReduceScatter.scratch(split),
+        ],
         compiler_params=comm_params(1), name="scatter_wgrad",
-    )(partial)
+    )(*args)
 
 
 def reduce_kernel(pieces, split, count, *refs):
-    sources, (act, weight, bias, out, mods, tiles, acc, load_sem, tile_sem), scratch = refs[:count], refs[count:count + 9], refs[count + 9:]
+    sources, (act, weight, bias, out, mods), scratch = refs[:count], refs[count:count + 5], refs[count + 5:]
     peers = Peers()
     peers.barrier()
-
-    def load(i):
-        slot = lax.rem(i, TWO)
-        local(weight.at[tile_at(i)], tiles.at[slot], load_sem.at[slot])
+    tiles, stages, scratch = Stream(*scratch[:TWO]), Stream(*scratch[TWO:ZS]), scratch[ZS:]
 
     def tile(i):
-        slot = lax.rem(i, TWO)
-
-        @pl.when(i >= TWO)
-        def _():
-            wait_for(acc.at[slot], tile_sem.at[slot])
-
-        @pl.when(i < TILES - 1)
-        def _():
-            load(i + 1)
-
-        wait_for(tiles.at[slot], load_sem.at[slot])
-        product = lax.dot_general(act[...], tiles[slot], CONTRACT_COLS, preferred_element_type=F32)
-        acc[slot] = (product + bias[:, tile_at(i)]).astype(BF16)
-        local(acc.at[slot], mods.at[:, tile_at(i)], tile_sem.at[slot])
-
-    load(0)
-    fill = Filler(tile, 3)
+        product = dot_cols(act[...], tiles.ready(i))
+        stages.store(i, (product + bias[:, tile_at(i)]).astype(BF16), mods.at[:, tile_at(i)])
+
+    fill = Filler([Job(TILES, tile, lambda i: tiles.load(i, weight.at[tile_at(i)]))], TWO)
+    fill.prime()
     own = len(AllGather.scratch)
     rs = ReduceScatter(peers, sources, pieces, split, scratch[own:])
     rs.run(fill)
     fill.finish()
     AllGather(peers, rs.part.at[peers.z, peers.y, peers.x], out, split, scratch[:own]).run()
     rs.drain()
-    drain_tiles(acc, tile_sem)
+    stages.drain()
 
 
 def reduce_all(sources, pieces, act, weight, bias):
@@ -575,7 +721,7 @@
         functools.partial(reduce_kernel, pieces, split, len(sources)),
         out_shape=[jax.ShapeDtypeStruct((ZS, TWO, TWO, TWO, split.rows, WIDTH), F32), jax.ShapeDtypeStruct((ROWS, MOD), BF16)],
         in_specs=[ANY] * len(sources) + [IN_VMEM, ANY, IN_VMEM], out_specs=[ANY, ANY],
-        scratch_shapes=[pltpu.VMEM((TWO, TILE, WIDTH), BF16), pltpu.VMEM((TWO, ROWS, TILE), BF16), DMA((TWO,)), DMA((TWO,)), *AllGather.scratch] + ReduceScatter.scratch(split),
+        scratch_shapes=[*Stream.scratch(BF16, TILE, WIDTH), *Stream.scratch(BF16, ROWS, TILE), *AllGather.scratch, *ReduceScatter.scratch(split)],
         compiler_params=comm_params(TWO), name="reduce_embed",
     )(*sources, act, weight, bias)
 
@@ -604,20 +750,20 @@
     )(total)
 
 
-def outer_kernel(left, right, out):
-    out[...] = lax.dot_general(left[...], right[...], CONTRACT_ROWS, preferred_element_type=F32)
-
-
-def outer(left, right):
-    rows, n = left.shape
+def compact_kernel(blocks, out):
+    for k in range(ZS):
+        out[k * SHARE:(k + 1) * SHARE] = blocks[k, :SHARE]
+
+
+def compact(blocks):
     return pl.pallas_call(
-        outer_kernel,
-        grid=(n // rows,),
-        out_shape=jax.ShapeDtypeStruct((n, WIDTH), F32),
-        in_specs=[pl.BlockSpec((rows, rows), lambda i: (0, i)), pl.BlockSpec((rows, WIDTH), lambda i: (0, 0))],
-        out_specs=pl.BlockSpec((rows, WIDTH), lambda i: (i, 0)),
-        compiler_params=pltpu.CompilerParams(vmem_limit_bytes=VMEM_LIMIT), name="outer",
-    )(left, right)
+        compact_kernel,
+        grid=(DEVICES // ZS,),
+        out_shape=jax.ShapeDtypeStruct((MOD, WIDTH), BF16),
+        in_specs=[pl.BlockSpec((ZS, PADDED, WIDTH), lambda i: (i, 0, 0))],
+        out_specs=pl.BlockSpec((ZS * SHARE, WIDTH), lambda i: (i, 0)),
+        compiler_params=pltpu.CompilerParams(vmem_limit_bytes=VMEM_LIMIT), name="compact",
+    )(blocks)
 
 
 def sinusoid(values, freq_width):
@@ -637,19 +783,6 @@
     act_bf = jax.nn.silu(hidden).astype(BF16)
     output = jnp.dot(act_bf, params[2], preferred_element_type=F32) + params[3].astype(F32)
     return output, hidden, act_bf
-
-
-def mlp_backward(inputs_bf, params, hidden, act_bf, d_out_bf):
-    grad_w2 = lax.dot_general(act_bf, d_out_bf, CONTRACT_ROWS, preferred_element_type=F32)
-    d_act = lax.dot_general(d_out_bf, params[2], CONTRACT_COLS, preferred_element_type=F32)
-    d_hidden = d_act * silu_grad(hidden)
-    d_hidden_bf = d_hidden.astype(BF16)
-    if inputs_bf.shape[1] > d_hidden_bf.shape[1]:
-        grad_w1 = outer(inputs_bf, d_hidden_bf)
-    else:
-        grad_w1 = lax.dot_general(inputs_bf, d_hidden_bf, CONTRACT_ROWS, preferred_element_type=F32)
-    grad_b1 = jnp.sum(d_hidden, axis=0)
-    return grad_w1, grad_b1, grad_w2
 
 
 def by_chip(grad):
@@ -683,24 +816,19 @@
         extra = jnp.pad(b_mod[None, :], ((0, PADDED - SHARE - 1), (0, WIDTH - SHARE)))
         gathered, part_wgrad = gather_blocks(jnp.concatenate([w_mod.T, extra], axis=0), d_mods, cond_silu)
         gathered = gathered.reshape(DEVICES, PADDED, WIDTH)
-        full_wt = gathered[:, :SHARE].reshape(MOD, WIDTH)
+        full_wt = compact(gathered)
         full_b = gathered[:, SHARE, :SHARE].reshape(1, MOD).astype(F32)
-        wgrad = scatter_sum(by_chip(part_wgrad), WGRAD_PIECES)
+        hidden, acts = [record[1] for record in saved], [record[2] for record in saved]
+        second = [params[TWO] for params in params_list]
+        wgrad, sums, *grads = scatter_sum(by_chip(part_wgrad), d_mods, full_wt, cond_vec, hidden, second, inputs_list, acts, WGRAD_PIECES)
         grad_wmod = lax.dynamic_slice(wgrad, (4 * lax.rem(me, TWO), 0), (SHARE, WIDTH)).T
-
-        d_cond = jnp.dot(d_mods, full_wt, preferred_element_type=F32)
-        d_vec = d_cond * silu_grad(cond_vec)
-        d_vec_bf = d_vec.astype(BF16)
-        grads = [mlp_backward(u, params, record[1], record[2], d_vec_bf) for u, params, record in zip(inputs_list, params_list, saved)]
-        bgrad_rows = MOD // WIDTH
+        bgrad_rows, count = MOD // WIDTH, len(hidden)
         part_bgrad = jnp.sum(d_mods, axis=0, dtype=F32).reshape(bgrad_rows, WIDTH)
-        vectors = [g[1] for g in grads] + [jnp.sum(d_vec, axis=0)]
-        vectors = jnp.concatenate([jnp.stack(vectors), part_bgrad], axis=0)
+        vectors = jnp.concatenate([sums[:ZS], part_bgrad], axis=0)
         vectors = jnp.pad(vectors, ((0, 128 - vectors.shape[0]), (0, 0)))
-        sources = [by_chip(g) for g in [g[0] for g in grads] + [g[2] for g in grads] + [vectors]]
+        sources = [by_chip(g) for g in (*grads, vectors)]
         total, modulation = reduce_all(sources, EMBED_PIECES, cond_silu, full_wt, full_b)
         *full, sums = [g.reshape(-1, WIDTH) for g in unpack(total, sources, EMBED_PIECES)]
-        count = len(grads)
         grad_bmod = lax.dynamic_slice(sums[ZS:ZS + bgrad_rows].reshape(MOD), (SHARE * me,), (SHARE,))
         embed_grads = [g for i in range(count) for g in (full[i], sums[i], full[i + count], sums[count])]
         return (modulation, grad_wmod, grad_bmod, *embed_grads)

time: 577 us -> 534 us (0.925)
  matrix products: 52.3 us -> 16.3 us
  local copies, waits for them, and re-layouts: 34.3 us -> 14.2 us
  Pallas kernels: 467 us -> 478 us
    dot_general x9 -> x0, matrix products: 40.3 us -> none  [the longest x1 14 us: local_step(): d_cond = jnp.dot(d_mods, full_wt, preferred_element_type=F32)]
    reshape x1 -> x0, local copies, waits for them, and re-layouts: 16.4 us -> none  [local_step(): full_wt = gathered[:, :SHARE].reshape(MOD, WIDTH)]
    pallas_call x1, Pallas kernels: 241 us -> 250 us  [reduce_all(): pl.pallas_call(functools.partial(reduce_kernel, pieces, split, len(source...]
    pallas_call x2, Pallas kernels: 131 us -> 137 us  [the longest x1 125 us: scatter_sum(): pl.pallas_call(functools.partial(scatter_kernel, pieces, split, len(hidde...]
where the time goes in v2:
time: 534 us; the launch traced here: 525 us
  Pallas kernels  478 us (90%)
  matrix products  16.3 us (3%)
  other arithmetic  15.2 us (3%)
  local copies, waits for them, and re-layouts  14.2 us (3%)
    pallas_call x1, Pallas kernels, reduce_all(): pl.pallas_call(functools.partial(reduce_kernel, pieces, split, len(source...  250 us
    pallas_call x1, Pallas kernels, scatter_sum(): pl.pallas_call(functools.partial(scatter_kernel, pieces, split, len(hidde...  125 us
    pallas_call x1, Pallas kernels, gather_blocks(): pl.pallas_call(functools.partial(gather_kernel, split), out_shape=[jax.Sh...  72.6 us
    pallas_call x1, Pallas kernels, unpack(): pl.pallas_call(functools.partial(unpack_kernel, pieces), out_shape=[jax.S...  18.6 us
    pallas_call x1, Pallas kernels, compact(): pl.pallas_call(compact_kernel, grid=(DEVICES // ZS,), out_shape=jax.Shape...  12 us

profile of v2, /device:TPU:0, one launch (start us, length us, event | category | flops | bytes accessed | tf_op | source)
XLA Modules:
  0.0 524.6 jit_solution(16157362205005550305)
XLA Ops:
  0.6 0.0 copy-start
  0.7 0.7 broadcast_in_dim.2
  1.4 0.7 broadcast_multiply_fusion.1
  2.1 0.7 broadcast_multiply_fusion
  2.8 0.7 convert_element_type.44
  3.5 0.7 convert_element_type.46
  4.1 0.7 convert_element_type.47
  4.8 0.7 convert_element_type.49
  5.5 0.7 convert_element_type.50
  6.2 0.7 convert_element_type.52
  6.9 4.0 convert_reduce_fusion
  10.9 0.0 copy-done.10
  10.9 0.8 fusion.3.own
  11.7 2.2 fusion.6
  14.0 0.9 pad_maximum_fusion
  14.8 0.0 copy-done
  14.8 2.2 multiply_convert_fusion.2
  17.0 2.2 multiply_convert_fusion.3
  19.1 0.9 copy-done.2
  20.0 1.9 convolution_add_fusion.5
  21.9 0.0 copy-done.6
  21.9 0.0 copy-done.7
  21.9 0.0 copy-done.3
  21.9 0.0 copy-start.5
  21.9 0.0 slice-start.1
  21.9 1.9 fusion.1
  23.8 0.0 slice-done
  23.9 0.0 copy-done.5
  23.9 0.0 slice-done.1
  23.9 0.0 copy-start.4
  23.9 4.5 multiply_convert_fusion.1
  28.4 3.7 multiply_convert_fusion
  32.1 72.6 %gather_wmod.1 = (bf16[4,2,2,2,184,1152]{5,4,3,2,1,0:T(8,128)(2,1)}, f32[5760,1152]{1,0:T(8,128)}) custom-call(bf16[184,1152]{1,0:T(8,128)(2,1)} %fusion.3.own, bf16[512,5760]{1,0:T(8,128)(2,1)} %refs_1_.1, bf16[512,1152]{1,0:T(8,128)(2,1)} %get-tuple-element.69.act.refs_7_), custom_call_target="tpu_custom_call" | custom-call | tf_op jit(solution)/shard_map/gather_wmod/pallas_call | solution.py:589
  104.7 1.0 fusion.8
  105.8 12.0 %compact.1.refs_2_.refs_8_ = bf16[5760,1152]{1,0:T(8,128)(2,1)} custom-call(bf16[32,184,1152]{2,1,0:T(8,128)(2,1)} %bitcast.31), custom_call_target="tpu_custom_call" | custom-call | tf_op jit(solution)/shard_map/compact/pallas_call | solution.py:759
  117.7 124.8 %scatter_wgrad.1 = (f32[184,1152]{1,0:T(8,128)}, f32[8,1152]{1,0:T(8,128)}, f32[256,1152]{1,0:T(8,128)}, f32[256,1152]{1,0:T(8,128)}, f32[2048,1152]{1,0:T(8,128...) custom-call(f32[4,2,2,360,1152]{4,3,2,1,0:T(8,128)} %bitcast.29, bf16[512,5760]{1,0:T(8,128)(2,1)} %refs_1_.1, ...), custom_call_target="tpu_custom_call" | custom-call | tf_op jit(solution)/shard_map/scatter_wgrad/pallas_call | solution.py:684
  242.5 0.8 reshape.129.refs_9_
  243.3 0.8 slice.23
  244.1 0.9 select_maximum_fusion
  244.9 249.6 %reduce_embed.1 = (f32[4,2,2,2,192,1152]{5,4,3,2,1,0:T(8,128)}, bf16[512,5760]{1,0:T(8,128)(2,1)}) custom-call(f32[4,2,2,16,1152]{4,3,2,1,0:T(8,128)} %bitcast.37, f32[4,2,2,16,1152]{4,3,2,1,0:T(8,128)} %bitcast.38, f32[4,2,2,128,1152]{4,3,2,1,0:T(8,128)} %bitcast.32, f32[4,2,2,72,1152]{4,3,2,1,0:T(8,128)} %bitcast.33, f32[4,2,2,72,1152]{4,3,2,1,0:T(8,128)} %bitcast.34, ...), custom_call_target="tpu_custom_call" | custom-call | tf_op jit(solution)/shard_map/reduce_embed/pallas_call | solution.py:720
  494.5 1.0 dynamic-slice_bitcast_fusion
  495.5 18.6 %unpack.1 = (f32[4,2,2,16,1152]{4,3,2,1,0:T(8,128)}, f32[4,2,2,16,1152]{4,3,2,1,0:T(8,128)}, f32[4,2,2,128,1152]{4,3,2,1,0:T(8,128)}, f32[4,2,2,72,1152]{4,3,2,1...) custom-call(f32[4,2,2,2,192,1152]{5,4,3,2,1,0:T(8,128)} %get-tuple-elemen, ...), custom_call_target="tpu_custom_call" | custom-call | tf_op jit(solution)/shard_map/unpack/pallas_call | solution.py:744
  514.1 1.6 slice_reduce_fusion
  515.7 0.9 slice.31
  516.6 0.6 dynamic_slice.7
  517.2 0.6 copy.36
  517.8 0.6 copy.37
  518.4 5.7 %copy.38 = bf16[512,5760]{1,0:T(8,128)(2,1)} copy(bf16[512,5760]{1,0:T(8,128)(2,1)} %get-tuple-element.118) | data formatting | bytes 11796480
  (21 shorter events, 0.1 us)
Async XLA Ops:
  0.6 14.2 %copy-start = (bf16[256,1152]{1,0:T(8,128)(2,1)S(1)}, bf16[256,1152]{1,0:T(8,128)(2,1)}, u32[]{:S(2)}) copy-start(bf16[256,1152]{1,0:T(8,128)(2,1)} %param.25) | copy-start | bytes 1769476
  6.9 4.0 copy-start.10
  14.8 2.2 copy-start.12
  17.0 4.9 copy-start.6
  17.0 3.0 copy-start.2
  19.1 2.7 copy-start.7
  20.0 1.9 copy-start.3
  20.0 3.8 slice-start
  21.9 2.0 copy-start.5
  21.9 2.0 slice-start.1
  23.9 4.5 copy-start.4
  28.4 3.7 copy-start.8
  244.9 249.6 %copy-start.9 = (f32[184,1152]{1,0:T(8,128)S(1)}, f32[184,1152]{1,0:T(8,128)}, u32[]{:S(2)}) copy-start(f32[184,1152]{1,0:T(8,128)} %get-tuple-element.44) | copy-start | bytes 2543620
  515.7 8.5 %copy-start.11 = (f32[1152]{0:T(1024)}, f32[1152]{0:T(1024)S(1)}, u32[]{:S(2)}) copy-start(f32[1152]{0:T(1024)S(1)} %get-tuple-element.124) | copy-start | bytes 13828
  518.4 5.7 %copy-start.1 = (bf16[256,1152]{1,0:T(8,128)(2,1)S(1)}, bf16[256,1152]{1,0:T(8,128)(2,1)}, u32[]{:S(2)}) copy-start(bf16[256,1152]{1,0:T(8,128)(2,1)} %param.25) | copy-start | bytes 1769476

commit v3 on v2

--- a/solution.py
+++ b/solution.py
@@ -444,12 +444,19 @@
         self.at_distance(0, self.finish)
         fill()
         self.at_distance(near, self.relay)
+        fill()
         self.at_distance(far, self.arrive)
         fill()
         self.at_distance(near, self.finish)
-        self.at_distance(mid, self.relay, self.finish)
+        fill()
+        self.at_distance(mid, self.relay)
+        fill()
+        self.at_distance(mid, self.finish)
+        fill()
         self.at_distance(far, self.relay)
+        fill()
         p.elsewhere(self.band_in)
+        fill()
         self.at_distance(far, self.finish)
         self.slab.drain()
         p.elsewhere(lambda zp: wait_for(self.band(zp), self.bsems[zp][0]))
@@ -467,8 +474,8 @@
 
 
 class Job:
-    def __init__(self, count, body, load=None):
-        self.count, self.body, self.load = count, body, load
+    def __init__(self, count, body, load=None, close=None):
+        self.count, self.body, self.load, self.close = count, body, load, close
 
 
 class Filler:
@@ -481,6 +488,12 @@
     def part(self, stop):
         job, last = self.jobs[self.job], self.jobs[self.job].count - 1
         after = next((j.load for j in self.jobs[self.job + 1:] if j.load), None)
+
+        def next_job():
+            if job.close:
+                job.close()
+            if after:
+                after(0)
 
         def tile(i, carry):
             if job.load:
@@ -488,9 +501,11 @@
                 def _():
                     job.load(i + 1)
 
-                if after:
-                    pl.when(i == last)(lambda: after(0))
+                if not job.close:
+                    pl.when(i == last)(next_job)
             job.body(i)
+            if job.close:
+                pl.when(i == last)(next_job)
             return carry
 
         lax.fori_loop(self.at, stop, tile, 0)
@@ -527,13 +542,12 @@
         wait_for(self.buf.at[slot], self.sems.at[slot])
         return self.buf[slot]
 
+    def free(self, i):
+        pl.when(i + self.base >= TWO)(lambda: wait_for(self.buf.at[self.slot(i)], self.sems.at[self.slot(i)]))
+
     def store(self, i, value, dst):
         slot = self.slot(i)
-
-        @pl.when(i + self.base >= TWO)
-        def _():
-            wait_for(self.buf.at[slot], self.sems.at[slot])
-
+        self.free(i)
         self.buf[slot] = value
         local(self.buf.at[slot], dst, self.sems.at[slot])
 
@@ -541,6 +555,9 @@
         for slot in range(TWO):
             wait_for(self.buf.at[slot], self.sems.at[slot])
 
+    def trim(self, *at):
+        return Stream(self.buf.at[(slice(None), *at)], self.sems)
+
     def after(self, count):
         return Stream(self.buf, self.sems, self.base + count)
 
@@ -550,7 +567,7 @@
 
 
 def tile_at(i, width=TILE, start=0):
-    return pl.ds(pl.multiple_of(start + i * width, 128), width)
+    return pl.ds(pl.multiple_of(start + i * width, 16 if width % 128 else 128), width)
 
 
 def dot_rows(left, right):
@@ -565,48 +582,100 @@
     return pltpu.CompilerParams(collective_id=ident, has_side_effects=True, vmem_limit_bytes=VMEM_LIMIT)
 
 
-def gather_kernel(split, own, d_mods, act, out, wgrad, mods, load_sem, *scratch):
-    local(d_mods, mods, load_sem)
+def gather_kernel(split, mlps, own, d_mods, biases, *refs):
+    refs = list(refs)
+    take = lambda n: [refs.pop(0) for _ in range(n)]
+    sources = [d_mods, *take(3 * mlps)]
+    out, wgrad, bgrad = take(3)
+    results, hidden = take(mlps + TWO), take(mlps)
+    mods, *weights = take(len(sources))
+    kept = take(len(results))
+    cvec, act, *acts = kept
+    load_sem, keep_sem = take(TWO)
+    inputs, first, second = weights[:mlps], weights[mlps:TWO * mlps], weights[TWO * mlps:]
+    tiles, stages = Stream(*take(TWO)), Stream(*take(TWO))
+    pairs = list(zip(sources, [mods, *weights]))
+    for n, (src, dst) in enumerate(pairs[1:] + pairs[:1]):
+        local(src, dst, load_sem.at[n])
     peers = Peers()
     peers.barrier()
-    tiles, scratch = Stream(*scratch[:TWO]), scratch[TWO:]
+
+    def ready(i, buf, n):
+        pl.when(i == 0)(lambda: wait_for(buf, load_sem.at[n]))
+
+    jobs = []
+    per = WIDTH // TILE
+    for k in range(mlps):
+        def hide(i, k=k, stage=stages.after(k * per)):
+            ready(i, inputs[k], k)
+            ready(i, first[k], k + mlps)
+            value = jnp.dot(inputs[k][...], first[k][:, tile_at(i)], preferred_element_type=F32) + biases[k:k + 1, tile_at(i)]
+            stage.store(i, value, hidden[k].at[:, tile_at(i)])
+            acts[k][:, tile_at(i)] = jax.nn.silu(value).astype(BF16)
+
+        jobs.append(Job(per, hide))
+    for k in range(mlps):
+        def embed(i, k=k):
+            ready(i, second[k], k + TWO * mlps)
+            value = jnp.dot(acts[k][...], second[k][:, tile_at(i)], preferred_element_type=F32) + biases[k + mlps:k + mlps + 1, tile_at(i)]
+            cvec[:, tile_at(i)] = cvec[:, tile_at(i)] + value if k else value
+
+        jobs.append(Job(per, embed))
+
+    def activate(i):
+        at = tile_at(i, ROWS // ZS)
+        act[at, :] = jax.nn.silu(cvec[at, :]).astype(BF16)
+
+    def keep():
+        for n, (src, dst) in enumerate(zip(kept, results)):
+            local(src, dst, keep_sem.at[n])
 
     def tile(i):
-        @pl.when(i == 0)
-        def _():
-            wait_for(mods, load_sem)
-
-        tiles.store(i, dot_rows(mods[:, tile_at(i)], act[...]), wgrad.at[tile_at(i)])
-
-    fill = Filler([Job(TILES, tile)], TWO)
-    AllGather(peers, own, out, split, scratch).run(fill)
+        ready(i, mods, len(weights))
+        left = mods[:, tile_at(i)]
+        bgrad[:, tile_at(i)] = jnp.sum(left.astype(F32), axis=0, keepdims=True)
+        tiles.store(i, dot_rows(left, act[...]), wgrad.at[tile_at(i)])
+
+    fill = Filler(jobs + [Job(ZS, activate, close=keep), Job(TILES, tile)], 3)
+    AllGather(peers, own, out, split, refs).run(fill)
     fill.finish()
     tiles.drain()
-
-
-def gather_blocks(block, d_mods, act):
-    split = Split(*WMOD_SPLIT)
+    stages.drain()
+    for n, buf in enumerate(kept):
+        wait_for(buf, keep_sem.at[n])
+
+
+def gather_blocks(block, d_mods, biases, inputs, first, second):
+    split, mlps = Split(*WMOD_SPLIT), len(inputs)
+    sources = [*inputs, *first, *second]
+    wide = (ROWS, WIDTH)
+    kept = [(wide, F32)] + [(wide, BF16)] * (mlps + 1)
+    shapes = [(MOD, WIDTH), (1, MOD)]
     return pl.pallas_call(
-        functools.partial(gather_kernel, split),
-        out_shape=[jax.ShapeDtypeStruct((ZS, TWO, TWO, TWO, split.rows, WIDTH), block.dtype), jax.ShapeDtypeStruct((MOD, WIDTH), F32)],
-        in_specs=[ANY, ANY, IN_VMEM], out_specs=[ANY, ANY],
-        scratch_shapes=[pltpu.VMEM(d_mods.shape, BF16), DMA, *Stream.scratch(F32, TILE, WIDTH), *AllGather.scratch],
+        functools.partial(gather_kernel, split, mlps),
+        out_shape=[jax.ShapeDtypeStruct((ZS, TWO, TWO, TWO, split.rows, WIDTH), block.dtype)]
+        + [jax.ShapeDtypeStruct(shape, F32) for shape in shapes] + [jax.ShapeDtypeStruct(*k) for k in kept] + [jax.ShapeDtypeStruct(wide, F32)] * mlps,
+        in_specs=[ANY, ANY, IN_VMEM] + [ANY] * len(sources), out_specs=[ANY, ANY, IN_VMEM] + [ANY] * (len(kept) + mlps),
+        scratch_shapes=[
+            *(pltpu.VMEM(a.shape, BF16) for a in (d_mods, *sources)), *(pltpu.VMEM(*k) for k in kept), DMA((len(sources) + 1,)), DMA((len(kept),)),
+            *Stream.scratch(F32, TILE, WIDTH), *Stream.scratch(F32, ROWS, TILE), *AllGather.scratch,
+        ],
         compiler_params=comm_params(0), name="gather_wmod",
-    )(block, d_mods, act)
+    )(block, d_mods, biases, *sources)
 
 
 def scatter_kernel(pieces, split, mlps, *refs):
     refs = list(refs)
     take = lambda n: [refs.pop(0) for _ in range(n)]
-    source, d_mods, weight, cond = take(ZS)
+    source, d_mods, blocks, cond = take(ZS)
     hidden, second, inputs, acts = (take(mlps) for _ in range(ZS))
-    out, sums = take(TWO)
+    out, sums, weight = take(3)
     grads1, grads2 = take(mlps), take(mlps)
-    mods, dcond, cvec, sem, mods_sem, cond_sem = take(6)
-    wtiles, htiles, ltiles, stiles, lsmall, ssmall = (Stream(*take(TWO)) for _ in range(6))
-    small = lsmall.buf.shape[-1]
+    mods, dcond, sem, mods_sem = take(ZS)
+    wtiles, htiles, ltiles, stiles, padded, packed = (Stream(*take(TWO)) for _ in range(6))
+    small = inputs[0].shape[1]
+    lsmall, ssmall = ltiles.trim(slice(None), pl.ds(0, small)), stiles.trim(pl.ds(0, small))
     local(d_mods, mods, mods_sem)
-    local(cond, cvec, cond_sem)
     peers = Peers()
     peers.barrier()
     rs = ReduceScatter(peers, [source], pieces, split, refs)
@@ -625,18 +694,26 @@
     def d_vec(i):
         @pl.when(i == 0)
         def _():
-            wait_for(cvec, cond_sem)
             sums[...] = jnp.zeros_like(sums)
 
-        at = tile_at(i, small)
-        value = dcond[at, :] * silu_grad(cvec[at, :])
-        mods[at, :WIDTH] = value.astype(BF16)
-        sums[mlps:mlps + 1, :] += jnp.sum(value, axis=0, keepdims=True)
+        at = tile_at(i)
+        value = dcond[:, at] * silu_grad(htiles.ready(i))
+        mods[:, at] = value.astype(BF16)
+        sums[mlps:mlps + 1, at] = jnp.sum(value, axis=0, keepdims=True)
+
+    def pack(i):
+        slot = packed.slot(i)
+        padded.ready(i)
+        packed.free(i)
+        for k in range(ZS):
+            packed.buf[slot, k * SHARE:(k + 1) * SHARE] = padded.buf[slot, k, :SHARE]
+        local(packed.buf.at[slot], weight.at[tile_at(i, ZS * SHARE)], packed.sems.at[slot])
 
     per = WIDTH // TILE
-    jobs = [Job(TILES, d_cond, lambda i: wtiles.load(i, weight.at[tile_at(i)])), Job(ROWS // small, d_vec)]
+    jobs = [Job(DEVICES // ZS, pack, lambda i: padded.load(i, blocks.at[pl.ds(i * ZS, ZS)]), packed.drain)]
+    jobs += [Job(TILES, d_cond, lambda i: wtiles.load(i, weight.at[tile_at(i)])), Job(per, d_vec, lambda i: htiles.load(i, cond.at[:, tile_at(i)]))]
     for k in range(mlps):
-        w, h = wtiles.after(TILES + k * per), htiles.after(k * per)
+        w, h = wtiles.after(TILES + k * per), htiles.after((k + 1) * per)
 
         def load(i, k=k, w=w, h=h):
             w.load(i, second[k].at[tile_at(i)])
@@ -649,18 +726,18 @@
 
         jobs.append(Job(per, d_hidden, load))
 
-    def outer(count, left, right, dst, lefts, stages, width):
+    def outer(count, left, right, dst, lefts, stages, width, close=None):
         def load(i):
             lefts.load(i, left.at[:, tile_at(i, width)])
 
         def body(i):
             stages.store(i, dot_rows(lefts.ready(i), right[...]), dst.at[tile_at(i, width)])
 
-        jobs.append(Job(count, body, load))
+        jobs.append(Job(count, body, load, close))
 
     done = 0
     for k in range(mlps):
-        outer(per, acts[k], vector(0), grads2[k], ltiles.after(k * per), stiles.after(k * per), TILE)
+        outer(per, acts[k], vector(0), grads2[k], ltiles.after(k * per), stiles.after(k * per), TILE, stiles.drain if k == mlps - 1 else None)
     for k in range(mlps):
         count = inputs[k].shape[1] // small
         outer(count, inputs[k], vector(k + 1), grads1[k], lsmall.after(done), ssmall.after(done), small)
@@ -670,35 +747,52 @@
     rs.run(fill)
     local(rs.part.at[peers.z, peers.y, peers.x], out, sem)
     fill.finish()
-    stiles.drain()
     ssmall.drain()
     rs.drain()
     wait_for(out, sem)
 
 
-def scatter_sum(partial, d_mods, weight, cond, hidden, second, inputs, acts, pieces):
+def scatter_sum(partial, d_mods, blocks, cond, hidden, second, inputs, acts, pieces):
     split = Split(*WGRAD_SPLIT)
-    args = [partial, d_mods, weight, cond, *hidden, *second, *inputs, *acts]
-    small = inputs[0].shape[1]
+    args = [partial, d_mods, blocks, cond, *hidden, *second, *inputs, *acts]
     grads = [jax.ShapeDtypeStruct((a.shape[1], WIDTH), F32) for a in (*inputs, *acts)]
     return pl.pallas_call(
         functools.partial(scatter_kernel, pieces, split, len(hidden)),
-        out_shape=[jax.ShapeDtypeStruct((split.rows, WIDTH), F32), jax.ShapeDtypeStruct((8, WIDTH), F32), *grads],
-        in_specs=[ANY] * len(args), out_specs=[ANY, IN_VMEM] + [ANY] * len(grads),
+        out_shape=[jax.ShapeDtypeStruct((split.rows, WIDTH), F32), jax.ShapeDtypeStruct((8, WIDTH), F32), jax.ShapeDtypeStruct((MOD, WIDTH), BF16), *grads],
+        in_specs=[ANY] * len(args), out_specs=[ANY, IN_VMEM] + [ANY] * (len(grads) + 1),
         scratch_shapes=[
-            pltpu.VMEM(d_mods.shape, BF16), pltpu.VMEM(cond.shape, F32), pltpu.VMEM(cond.shape, F32), DMA, DMA, DMA,
+            pltpu.VMEM(d_mods.shape, BF16), pltpu.VMEM(cond.shape, F32), DMA, DMA,
             *Stream.scratch(BF16, TILE, WIDTH), *Stream.scratch(F32, ROWS, TILE), *Stream.scratch(BF16, ROWS, TILE), *Stream.scratch(F32, TILE, WIDTH),
-            *Stream.scratch(BF16, ROWS, small), *Stream.scratch(F32, small, WIDTH), *ReduceScatter.scratch(split),
+            *Stream.scratch(BF16, ZS, PADDED, WIDTH), *Stream.scratch(BF16, ZS * SHARE, WIDTH), *ReduceScatter.scratch(split),
         ],
         compiler_params=comm_params(1), name="scatter_wgrad",
     )(*args)
 
 
 def reduce_kernel(pieces, split, count, *refs):
-    sources, (act, weight, bias, out, mods), scratch = refs[:count], refs[count:count + 5], refs[count + 5:]
+    sources, out, scratch = refs[:count], refs[count], refs[count + 1:]
     peers = Peers()
     peers.barrier()
-    tiles, stages, scratch = Stream(*scratch[:TWO]), Stream(*scratch[TWO:ZS]), scratch[ZS:]
+    own = len(AllGather.scratch)
+    rs = ReduceScatter(peers, sources, pieces, split, scratch[own:])
+    rs.run()
+    AllGather(peers, rs.part.at[peers.z, peers.y, peers.x], out, split, scratch[:own]).run()
+    rs.drain()
+
+
+def reduce_all(sources, pieces):
+    split = Split(*EMBED_SPLIT)
+    return pl.pallas_call(
+        functools.partial(reduce_kernel, pieces, split, len(sources)),
+        out_shape=jax.ShapeDtypeStruct((ZS, TWO, TWO, TWO, split.rows, WIDTH), F32),
+        in_specs=[ANY] * len(sources), out_specs=ANY, scratch_shapes=[*AllGather.scratch, *ReduceScatter.scratch(split)],
+        compiler_params=comm_params(TWO), name="reduce_embed",
+    )(*sources)
+
+
+def unpack_kernel(pieces, total, act, weight, bias, *refs):
+    mods, *outs, buf, load_sem, store_sem = refs[:-ZS]
+    tiles, stages = Stream(*refs[-ZS:-TWO]), Stream(*refs[-TWO:])
 
     def tile(i):
         product = dot_cols(act[...], tiles.ready(i))
@@ -706,28 +800,6 @@
 
     fill = Filler([Job(TILES, tile, lambda i: tiles.load(i, weight.at[tile_at(i)]))], TWO)
     fill.prime()
-    own = len(AllGather.scratch)
-    rs = ReduceScatter(peers, sources, pieces, split, scratch[own:])
-    rs.run(fill)
-    fill.finish()
-    AllGather(peers, rs.part.at[peers.z, peers.y, peers.x], out, split, scratch[:own]).run()
-    rs.drain()
-    stages.drain()
-
-
-def reduce_all(sources, pieces, act, weight, bias):
-    split = Split(*EMBED_SPLIT)
-    return pl.pallas_call(
-        functools.partial(reduce_kernel, pieces, split, len(sources)),
-        out_shape=[jax.ShapeDtypeStruct((ZS, TWO, TWO, TWO, split.rows, WIDTH), F32), jax.ShapeDtypeStruct((ROWS, MOD), BF16)],
-        in_specs=[ANY] * len(sources) + [IN_VMEM, ANY, IN_VMEM], out_specs=[ANY, ANY],
-        scratch_shapes=[*Stream.scratch(BF16, TILE, WIDTH), *Stream.scratch(BF16, ROWS, TILE), *AllGather.scratch, *ReduceScatter.scratch(split)],
-        compiler_params=comm_params(TWO), name="reduce_embed",
-    )(*sources, act, weight, bias)
-
-
-def unpack_kernel(pieces, total, *refs):
-    *outs, buf, load_sem, store_sem = refs
     order = [(zp, core) for zp in range(ZS) for core in range(TWO)]
     for at in order:
         local(total.at[at[0], :, :, at[1]], buf.at[at], load_sem.at[at])
@@ -736,34 +808,24 @@
         zp, core = at
         for dst, start, n, row in pieces[core]:
             local(buf.at[zp, core, :, :, pl.ds(row, n)], outs[dst].at[zp, :, :, pl.ds(start, n)], store_sem.at[at])
+        fill()
+    fill.finish()
+    stages.drain()
     for at in order:
         wait_for(buf.at[at], store_sem.at[at])
 
 
-def unpack(total, sources, pieces):
+def unpack(total, sources, pieces, act, weight, bias):
     return pl.pallas_call(
         functools.partial(unpack_kernel, pieces),
-        out_shape=[jax.ShapeDtypeStruct(s.shape, s.dtype) for s in sources],
-        in_specs=[ANY], out_specs=[ANY] * len(sources),
-        scratch_shapes=[pltpu.VMEM((ZS, TWO, TWO, TWO, *total.shape[ZS:]), F32), DMA((ZS, TWO)), DMA((ZS, TWO))],
+        out_shape=[jax.ShapeDtypeStruct((ROWS, MOD), BF16)] + [jax.ShapeDtypeStruct(s.shape, s.dtype) for s in sources],
+        in_specs=[ANY, IN_VMEM, ANY, IN_VMEM], out_specs=[ANY] * (len(sources) + 1),
+        scratch_shapes=[
+            pltpu.VMEM((ZS, TWO, TWO, TWO, *total.shape[ZS:]), F32), DMA((ZS, TWO)), DMA((ZS, TWO)),
+            *Stream.scratch(BF16, TILE, WIDTH), *Stream.scratch(BF16, ROWS, TILE),
+        ],
         compiler_params=pltpu.CompilerParams(vmem_limit_bytes=VMEM_LIMIT), name="unpack",
-    )(total)
-
-
-def compact_kernel(blocks, out):
-    for k in range(ZS):
-        out[k * SHARE:(k + 1) * SHARE] = blocks[k, :SHARE]
-
-
-def compact(blocks):
-    return pl.pallas_call(
-        compact_kernel,
-        grid=(DEVICES // ZS,),
-        out_shape=jax.ShapeDtypeStruct((MOD, WIDTH), BF16),
-        in_specs=[pl.BlockSpec((ZS, PADDED, WIDTH), lambda i: (i, 0, 0))],
-        out_specs=pl.BlockSpec((ZS * SHARE, WIDTH), lambda i: (i, 0)),
-        compiler_params=pltpu.CompilerParams(vmem_limit_bytes=VMEM_LIMIT), name="compact",
-    )(blocks)
+    )(total, act, weight, bias)
 
 
 def sinusoid(values, freq_width):
@@ -776,13 +838,6 @@
 def silu_grad(values):
     sigmoid_v = jax.nn.sigmoid(values)
     return sigmoid_v * (1.0 + values * (1.0 - sigmoid_v))
-
-
-def mlp_forward(inputs_bf, params):
-    hidden = jnp.dot(inputs_bf, params[0], preferred_element_type=F32) + params[1].astype(F32)
-    act_bf = jax.nn.silu(hidden).astype(BF16)
-    output = jnp.dot(act_bf, params[2], preferred_element_type=F32) + params[3].astype(F32)
-    return output, hidden, act_bf
 
 
 def by_chip(grad):
@@ -808,27 +863,25 @@
         me = lax.axis_index(AXIS)
         freq_width = time_w1.shape[0]
         inputs_list = [sinusoid(timesteps, freq_width), sinusoid(guidance, freq_width), pooled]
-        params_list = [(time_w1, time_b1, time_w2, time_b2), (guide_w1, guide_b1, guide_w2, guide_b2), (text_w1, text_b1, text_w2, text_b2)]
-        saved = [mlp_forward(u, params) for u, params in zip(inputs_list, params_list)]
-        cond_vec = saved[0][0] + saved[1][0] + saved[2][0]
-        cond_silu = jax.nn.silu(cond_vec).astype(BF16)
-
+        first, second = [time_w1, guide_w1, text_w1], [time_w2, guide_w2, text_w2]
+        count = len(first)
+        biases = jnp.stack([time_b1, guide_b1, text_b1, time_b2, guide_b2, text_b2]).astype(F32)
         extra = jnp.pad(b_mod[None, :], ((0, PADDED - SHARE - 1), (0, WIDTH - SHARE)))
-        gathered, part_wgrad = gather_blocks(jnp.concatenate([w_mod.T, extra], axis=0), d_mods, cond_silu)
+        block = jnp.concatenate([w_mod.T, extra], axis=0)
+        gathered, part_wgrad, part_bgrad, cond_vec, cond_silu, *rest = gather_blocks(block, d_mods, biases, inputs_list, first, second)
+        acts, hidden = rest[:count], rest[count:]
         gathered = gathered.reshape(DEVICES, PADDED, WIDTH)
-        full_wt = compact(gathered)
         full_b = gathered[:, SHARE, :SHARE].reshape(1, MOD).astype(F32)
-        hidden, acts = [record[1] for record in saved], [record[2] for record in saved]
-        second = [params[TWO] for params in params_list]
-        wgrad, sums, *grads = scatter_sum(by_chip(part_wgrad), d_mods, full_wt, cond_vec, hidden, second, inputs_list, acts, WGRAD_PIECES)
+        wgrad, sums, full_wt, *grads = scatter_sum(by_chip(part_wgrad), d_mods, gathered, cond_vec, hidden, second, inputs_list, acts, WGRAD_PIECES)
         grad_wmod = lax.dynamic_slice(wgrad, (4 * lax.rem(me, TWO), 0), (SHARE, WIDTH)).T
-        bgrad_rows, count = MOD // WIDTH, len(hidden)
-        part_bgrad = jnp.sum(d_mods, axis=0, dtype=F32).reshape(bgrad_rows, WIDTH)
+        bgrad_rows = MOD // WIDTH
+        part_bgrad = part_bgrad.reshape(bgrad_rows, WIDTH)
         vectors = jnp.concatenate([sums[:ZS], part_bgrad], axis=0)
         vectors = jnp.pad(vectors, ((0, 128 - vectors.shape[0]), (0, 0)))
         sources = [by_chip(g) for g in (*grads, vectors)]
-        total, modulation = reduce_all(sources, EMBED_PIECES, cond_silu, full_wt, full_b)
-        *full, sums = [g.reshape(-1, WIDTH) for g in unpack(total, sources, EMBED_PIECES)]
+        total = reduce_all(sources, EMBED_PIECES)
+        modulation, *full = unpack(total, sources, EMBED_PIECES, cond_silu, full_wt, full_b)
+        *full, sums = [g.reshape(-1, WIDTH) for g in full]
         grad_bmod = lax.dynamic_slice(sums[ZS:ZS + bgrad_rows].reshape(MOD), (SHARE * me,), (SHARE,))
         embed_grads = [g for i in range(count) for g in (full[i], sums[i], full[i + count], sums[count])]
         return (modulation, grad_wmod, grad_bmod, *embed_grads)

time: 534 us -> 495 us (0.927)
  matrix products: 16.3 us -> 0 us
  Pallas kernels: 478 us -> 469 us
  other arithmetic: 15.2 us -> 8.78 us
    dot_general x6 -> x0, matrix products: 16.3 us -> none  [the longest x3 8.83 us: mlp_forward(): jnp.dot(inputs_bf, params[0], preferred_element_type=F32)]
    pallas_call x1, Pallas kernels: 250 us -> 236 us  [reduce_all(): pl.pallas_call(functools.partial(reduce_kernel, pieces, split, len(source...]
    pallas_call x1, Pallas kernels: 18.6 us -> 31.8 us  [unpack(): pl.pallas_call(functools.partial(unpack_kernel, pieces), out_shape=[jax.S...]
    pallas_call x2 -> x1, Pallas kernels: 84.6 us -> 73.7 us  [gather_blocks(): pl.pallas_call(functools.partial(gather_kernel, split, mlps), out_shape=[...]
    unnamed x33 -> x8, local copies, waits for them, and re-layouts: 7.84 us -> 1.21 us
where the time goes in v3:
time: 495 us; the launch traced here: 491 us
  Pallas kernels  469 us (95%)
  local copies, waits for them, and re-layouts  11.7 us (2%)
  other arithmetic  8.78 us (2%)
    pallas_call x1, Pallas kernels, reduce_all(): pl.pallas_call(functools.partial(reduce_kernel, pieces, split, len(source...  236 us
    pallas_call x1, Pallas kernels, scatter_sum(): pl.pallas_call(functools.partial(scatter_kernel, pieces, split, len(hidde...  128 us
    pallas_call x1, Pallas kernels, gather_blocks(): pl.pallas_call(functools.partial(gather_kernel, split, mlps), out_shape=[...  73.7 us
    pallas_call x1, Pallas kernels, unpack(): pl.pallas_call(functools.partial(unpack_kernel, pieces), out_shape=[jax.S...  31.8 us

profile of v3, /device:TPU:0, one launch (start us, length us, event | category | flops | bytes accessed | tf_op | source)
XLA Modules:
  0.0 490.7 jit_solution(5278614344296786929)
XLA Ops:
  0.6 0.7 broadcast_multiply_fusion
  1.3 0.7 broadcast_multiply_fusion.1
  2.0 2.2 fusion.4
  4.2 0.8 pad_maximum_fusion
  5.1 0.7 broadcast_in_dim.2
  5.8 1.8 fusion.1.own
  7.6 0.7 stack.21
  8.2 0.7 stack.22
  8.9 0.7 stack.23
  9.6 0.7 stack.24
  10.3 0.7 stack.25
  11.0 0.7 stack.26
  11.7 0.1 stack.27
  11.8 0.6 convert_element_type.14.biases
  12.4 73.7 %gather_wmod.1 = (bf16[4,2,2,2,184,1152]{5,4,3,2,1,0:T(8,128)(2,1)}, f32[5760,1152]{1,0:T(8,128)}, f32[1,5760]{1,0:T(1,128)}, f32[512,1152]{1,0:T(8,128)}, bf16[...) custom-call(bf16[184,1152]{1,0:T(8,128)(2,1)} %fusion.1.own, ...), custom_call_target="tpu_custom_call" | custom-call | tf_op jit(solution)/shard_map/gather_wmod/pallas_call | solution.py:654
  86.1 0.0 copy-start.2
  86.1 128.2 %scatter_wgrad.1 = (f32[184,1152]{1,0:T(8,128)}, f32[8,1152]{1,0:T(8,128)}, bf16[5760,1152]{1,0:T(8,128)(2,1)}, f32[256,1152]{1,0:T(8,128)}, f32[256,1152]{1,0:T...) custom-call(f32[4,2,2,360,1152]{4,3,2,1,0:T(8,128)} %bitcast.19, ...), custom_call_target="tpu_custom_call" | custom-call | tf_op jit(solution)/shard_map/scatter_wgrad/pallas_call | solution.py:759
  214.3 0.8 slice.23
  215.1 0.0 copy-done.2
  215.1 0.1 reduce
  215.2 0.9 select_maximum_fusion
  216.1 235.7 %reduce_embed.1.total = f32[4,2,2,2,192,1152]{5,4,3,2,1,0:T(8,128)} custom-call(f32[4,2,2,16,1152]{4,3,2,1,0:T(8,128)} %bitcast.27, f32[4,2,2,16,1152]{4,3,2,1,0:T(8,128)} %bitcast.28, f32[4,2,2,128,1152]{4,3,2,1,0:T(8,128)} %bitcast.22, f32[4,2,2,72,1152]{4,3,2,1,0:T(8,128)} %bitcast.23, f32[4,2,2,72,1152]{4,3,2,1,0:T(8,128)} %bitcast.24, ...), custom_call_target="tpu_custom_call" | custom-call | tf_op jit(solution)/shard_map/reduce_embed/pallas_call | solution.py:785
  451.8 1.0 fusion.6
  452.8 0.8 reshape.123.bias
  453.6 0.0 copy-start
  453.6 31.8 %unpack.1 = (bf16[512,5760]{1,0:T(8,128)(2,1)}, f32[4,2,2,16,1152]{4,3,2,1,0:T(8,128)}, f32[4,2,2,16,1152]{4,3,2,1,0:T(8,128)}, f32[4,2,2,128,1152]{4,3,2,1,0:T(...) custom-call(f32[4,2,2,2,192,1152]{5,4,3,2,1,0:T(8,128)} %reduce_embe, ...), custom_call_target="tpu_custom_call" | custom-call | tf_op jit(solution)/shard_map/unpack/pallas_call | solution.py:819
  485.4 0.9 slice.31
  486.3 0.6 dynamic_slice.7
  486.9 1.6 slice_reduce_fusion
  488.5 0.0 copy-start.1
  488.5 0.0 copy-done
  488.5 1.0 dynamic-slice_bitcast_fusion
  489.5 0.6 copy.35
  490.1 0.6 copy.36
  490.7 0.0 copy-done.1
  (3 shorter events, 0.0 us)
Async XLA Ops:
  86.1 129.0 %copy-start.2 = (f32[1,5760]{1,0:T(1,128)S(1)}, f32[1,5760]{1,0:T(1,128)}, u32[]{:S(2)}) copy-start(f32[1,5760]{1,0:T(1,128)} %get-tuple-element.59) | copy-start | bytes 69124
  453.6 34.9 %copy-start = (f32[184,1152]{1,0:T(8,128)S(1)}, f32[184,1152]{1,0:T(8,128)}, u32[]{:S(2)}) copy-start(f32[184,1152]{1,0:T(8,128)} %get-tuple-element.63) | copy-start | bytes 2543620
  488.5 2.2 copy-start.1

commit v4 on v3

--- a/solution.py
+++ b/solution.py
@@ -106,6 +106,11 @@
         return [DMA(shape), DMA(shape)]
 
 
+def halves(start, size):
+    one = -(-size // CHIPS) * 8
+    return pl.ds(start, one), pl.ds(start + one, size - one)
+
+
 class Split:
     def __init__(self, *n):
         starts = [sum(n[:i]) for i in range(ZS)]
@@ -114,8 +119,7 @@
         self.a, self.b = sum(self.n[0]), sum(self.n[1])
         self.rows = self.a + self.b
         self.all_a, self.all_b = pl.ds(0, self.a), pl.ds(self.a, self.b)
-        size = -(-self.a // DEVICES) * 8
-        self.chunks = [pl.ds(at, min(size, self.a - at)) for at in range(0, self.a, size)]
+        self.units = [halves(start, size) for start, size in zip(starts, self.n[0])]
 
 
 class PlaneReduce:
@@ -169,20 +173,23 @@
     @staticmethod
     def scratch(s):
         whole = [(n, TWO, TWO, s.rows) for n in (ZS, TWO)]
-        planes = [(ZS,) + shape for shape in PlaneReduce.shapes(s.n[0])] + PlaneReduce.shapes(s.n[1])
+        planes = [(ZS,) + shape for unit in s.units for shape in PlaneReduce.shapes([at.size for at in unit])] + PlaneReduce.shapes(s.n[1])
         shapes = whole + planes + [(TWO, ZS, s.a), (ZS, TWO, TWO, s.b)]
         buffers = [pltpu.VMEM(shape + (WIDTH,), F32) for shape in shapes]
-        return buffers + [DMA((ZS,))] + Sems.scratch(ZS) + Sems.scratch(ZS, ZS) + Sems.scratch(TWO, ZS, len(s.chunks)) + Sems.scratch(ZS) + Sems.scratch(ZS)
+        return buffers + [DMA((ZS,))] + Sems.scratch(ZS) + Sems.scratch(ZS, TWO, ZS) + Sems.scratch(TWO, ZS, TWO, TWO) + Sems.scratch(ZS) + Sems.scratch(ZS)
 
     def __init__(self, p, sources, pieces, s, scratch):
         self.p, self.sources, self.pieces, self.s = p, sources, pieces, s
         scratch = list(scratch)
         take = lambda n: [scratch.pop(0) for _ in range(n)]
         self.part, self.own = take(TWO)
-        boxes, slab_boxes = take(ZS), take(ZS)
+        boxes, slab_boxes = [take(ZS) for _ in s.units], take(ZS)
         self.line, self.slabs, self.lsem = take(3)
         self.csems, plane_sems, self.zsems, self.bsems, slab_sems = (Sems(take(TWO)) for _ in range(5))
-        self.planes = [PlaneReduce(p, self.part.at[zp], s.colours[0], [box.at[zp] for box in boxes], plane_sems.under(zp)) for zp in range(ZS)]
+        self.planes = {
+            (zp, n): PlaneReduce(p, self.part.at[zp], unit, [box.at[zp] for box in boxes[n]], plane_sems.under(zp).under(n))
+            for zp in range(ZS) for n, unit in enumerate(s.units)
+        }
         self.slab = PlaneReduce(p, self.part.at[p.z], s.colours[1], slab_boxes, slab_sems)
 
     def partner(self, zp):
@@ -223,32 +230,32 @@
         wait_for(self.slabs.at[zp], self.bsems[zp][1])
         add_rows(self.part.at[self.p.z, :, :, self.s.all_b], self.slabs.at[zp])
 
-    def line_in(self, way, zp, k, part):
+    def line_in(self, way, zp, n, k, part):
         box = self.line.at[way, zp, part]
-        wait_for(box, self.zsems.under(way).under(zp)[k][1])
+        wait_for(box, self.zsems.under(way).under(zp).under(n)[k][1])
         add_rows(self.part.at[zp, self.p.y, self.p.x, part], box)
 
-    def hop(self, zp, distance):
-        p = self.p
+    def hop(self, unit, distance):
+        p, (zp, n) = self.p, unit
 
         def go(way, step):
-            for k, part in enumerate(self.s.chunks):
+            for k, part in enumerate(self.s.units[n]):
                 if distance:
-                    self.line_in(way, zp, k, part)
-                remote(self.part.at[zp, p.y, p.x, part], self.line.at[way, zp, part], self.zsems.under(way).under(zp)[k], p.column(p.z + step))
+                    self.line_in(way, zp, n, k, part)
+                remote(self.part.at[zp, p.y, p.x, part], self.line.at[way, zp, part], self.zsems.under(way).under(zp).under(n)[k], p.column(p.z + step))
 
         last = ZS - 1
         for way, (step, at, todo) in enumerate(((1, distance, distance < zp), (-1, last - distance, last - distance > zp))):
             if todo:
                 pl.when(p.z == at)(functools.partial(go, way, step))
 
-    def final(self, zp):
+    def final(self, zp, n):
         @pl.when(self.p.z == zp)
         def _():
-            for k, part in enumerate(self.s.chunks):
+            for k, part in enumerate(self.s.units[n]):
                 for way, end in enumerate((0, ZS - 1)):
                     if zp != end:
-                        self.line_in(way, zp, k, part)
+                        self.line_in(way, zp, n, k, part)
 
     def drain(self):
         p = self.p
@@ -256,67 +263,55 @@
         p.elsewhere(lambda zp: wait_for(self.slabs.at[zp], self.bsems[zp][0]))
 
         def sent(way, zp):
-            for k, part in enumerate(self.s.chunks):
-                wait_for(self.line.at[way, zp, part], self.zsems.under(way).under(zp)[k][0])
+            for n, unit in enumerate(self.s.units):
+                for k, part in enumerate(unit):
+                    wait_for(self.line.at[way, zp, part], self.zsems.under(way).under(zp).under(n)[k][0])
 
         for zp in range(ZS):
             wait_for(self.part.at[zp], self.csems[zp][0])
-            self.planes[zp].drain()
+            for n in range(TWO):
+                self.planes[zp, n].drain()
             for way, cond in enumerate((p.z < zp, p.z > zp)):
                 pl.when(cond)(functools.partial(sent, way, zp))
 
-    def run(self, fill=lambda: None):
-        one, two, three, four = Z_ORDER
-        planes = self.planes
+    def run(self, fill, lag):
+        units = [(zp, n) for zp in Z_ORDER for n in range(TWO)]
+        planes = [self.planes[unit] for unit in units]
         for zp in Z_ORDER:
             self.partner(zp)
-        self.load(one)
-        self.load(two)
-        fill()
-        for zp, later in zip(Z_ORDER, (three, four, None, None)):
+        for zp in Z_ORDER[:TWO]:
+            self.load(zp)
+        fill()
+        ahead = 3
+        for n, zp in enumerate(Z_ORDER):
             self.both_cores(zp)
-            if later is None:
-                self.slab_out(zp)
-            else:
+            for plane in planes[n * TWO:min(n * TWO + TWO, ahead)]:
+                plane.start()
+            self.slab_out(zp)
+            for later in Z_ORDER[TWO:][n:n + 1]:
                 self.load(later)
-                planes[zp].start()
-                self.slab_out(zp)
             fill()
-        planes[one].middle()
-        planes[three].start()
-        fill()
-        planes[one].end()
-        self.hop(one, 0)
-        fill()
-        planes[two].middle()
-        planes[four].start()
-        fill()
-        planes[two].end()
-        self.hop(two, 0)
-        self.hop(one, 1)
-        fill()
-        planes[three].middle()
-        fill()
-        planes[three].end()
-        self.hop(three, 0)
-        self.hop(two, 1)
-        self.hop(one, TWO)
-        fill()
-        self.p.elsewhere(self.slab_sum)
-        self.slab.start()
-        fill()
-        planes[four].middle()
-        self.slab.middle()
-        fill()
-        planes[four].end()
-        self.hop(four, 0)
-        self.hop(three, 1)
-        self.hop(two, TWO)
-        self.hop(four, 1)
+        last = len(units) - 1
+        for u, plane in enumerate(planes):
+            plane.middle()
+            for later in planes[u + ahead:u + ahead + 1]:
+                later.start()
+            if u == last:
+                self.slab.middle()
+            fill()
+            plane.end()
+            for distance, unit in enumerate(units[u::-lag][:3]):
+                self.hop(unit, distance)
+            if u == last - 1:
+                self.p.elsewhere(self.slab_sum)
+                self.slab.start()
+            fill()
+        for unit in units[-lag:]:
+            self.hop(unit, 1)
         self.slab.end()
         fill()
-        for zp in Z_ORDER:
-            self.final(zp)
+        for unit in units:
+            self.final(*unit)
 
 
 class PlaneGather:
@@ -744,7 +739,7 @@
         done += count
     fill = Filler(jobs, ZS)
     fill.prime()
-    rs.run(fill)
+    rs.run(fill, TWO)
     local(rs.part.at[peers.z, peers.y, peers.x], out, sem)
     fill.finish()
     ssmall.drain()
@@ -770,62 +765,65 @@
 
 
 def reduce_kernel(pieces, split, count, *refs):
-    sources, out, scratch = refs[:count], refs[count], refs[count + 1:]
+    sources, (act, weight, bias, out, mods), scratch = refs[:count], refs[count:count + 5], refs[count + 5:]
     peers = Peers()
     peers.barrier()
+    tiles, stages, scratch = Stream(*scratch[:TWO]), Stream(*scratch[TWO:ZS]), scratch[ZS:]
+
+    def tile(i):
+        product = dot_cols(act[...], tiles.ready(i))
+        stages.store(i, (product + bias[:, tile_at(i)]).astype(BF16), mods.at[:, tile_at(i)])
+
+    fill = Filler([Job(TILES, tile, lambda i: tiles.load(i, weight.at[tile_at(i)]))], 1)
+    fill.prime()
     own = len(AllGather.scratch)
     rs = ReduceScatter(peers, sources, pieces, split, scratch[own:])
-    rs.run()
+    rs.run(fill, TWO)
+    fill.finish()
     AllGather(peers, rs.part.at[peers.z, peers.y, peers.x], out, split, scratch[:own]).run()
     rs.drain()
-
-
-def reduce_all(sources, pieces):
+    stages.drain()
+
+
+def reduce_all(sources, pieces, act, weight, bias):
     split = Split(*EMBED_SPLIT)
     return pl.pallas_call(
         functools.partial(reduce_kernel, pieces, split, len(sources)),
-        out_shape=jax.ShapeDtypeStruct((ZS, TWO, TWO, TWO, split.rows, WIDTH), F32),
-        in_specs=[ANY] * len(sources), out_specs=ANY, scratch_shapes=[*AllGather.scratch, *ReduceScatter.scratch(split)],
+        out_shape=[jax.ShapeDtypeStruct((ZS, TWO, TWO, TWO, split.rows, WIDTH), F32), jax.ShapeDtypeStruct((ROWS, MOD), BF16)],
+        in_specs=[ANY] * len(sources) + [IN_VMEM, ANY, IN_VMEM], out_specs=[ANY, ANY],
+        scratch_shapes=[*Stream.scratch(BF16, TILE, WIDTH), *Stream.scratch(BF16, ROWS, TILE), *AllGather.scratch, *ReduceScatter.scratch(split)],
         compiler_params=comm_params(TWO), name="reduce_embed",
-    )(*sources)
-
-
-def unpack_kernel(pieces, total, act, weight, bias, *refs):
-    mods, *outs, buf, load_sem, store_sem = refs[:-ZS]
-    tiles, stages = Stream(*refs[-ZS:-TWO]), Stream(*refs[-TWO:])
-
-    def tile(i):
-        product = dot_cols(act[...], tiles.ready(i))
-        stages.store(i, (product + bias[:, tile_at(i)]).astype(BF16), mods.at[:, tile_at(i)])
-
-    fill = Filler([Job(TILES, tile, lambda i: tiles.load(i, weight.at[tile_at(i)]))], TWO)
-    fill.prime()
+    )(*sources, act, weight, bias)
+
+
+def unpack_kernel(pieces, total, mods, *refs):
+    final_mods, *outs, buf, mods_buf, load_sem, store_sem, mods_sem = refs
     order = [(zp, core) for zp in range(ZS) for core in range(TWO)]
+    local(mods, mods_buf, mods_sem.at[0])
     for at in order:
         local(total.at[at[0], :, :, at[1]], buf.at[at], load_sem.at[at])
+    wait_for(mods_buf, mods_sem.at[0])
+    local(mods_buf, final_mods, mods_sem.at[1])
     for at in order:
         wait_for(buf.at[at], load_sem.at[at])
         zp, core = at
         for dst, start, n, row in pieces[core]:
             local(buf.at[zp, core, :, :, pl.ds(row, n)], outs[dst].at[zp, :, :, pl.ds(start, n)], store_sem.at[at])
-        fill()
-    fill.finish()
-    stages.drain()
     for at in order:
         wait_for(buf.at[at], store_sem.at[at])
-
-
-def unpack(total, sources, pieces, act, weight, bias):
+    wait_for(mods_buf, mods_sem.at[1])
+
+
+def unpack(total, mods, sources, pieces):
     return pl.pallas_call(
         functools.partial(unpack_kernel, pieces),
-        out_shape=[jax.ShapeDtypeStruct((ROWS, MOD), BF16)] + [jax.ShapeDtypeStruct(s.shape, s.dtype) for s in sources],
-        in_specs=[ANY, IN_VMEM, ANY, IN_VMEM], out_specs=[ANY] * (len(sources) + 1),
+        out_shape=[jax.ShapeDtypeStruct(s.shape, s.dtype) for s in (mods, *sources)],
+        in_specs=[ANY, ANY], out_specs=[ANY] * (len(sources) + 1),
         scratch_shapes=[
-            pltpu.VMEM((ZS, TWO, TWO, TWO, *total.shape[ZS:]), F32), DMA((ZS, TWO)), DMA((ZS, TWO)),
-            *Stream.scratch(BF16, TILE, WIDTH), *Stream.scratch(BF16, ROWS, TILE),
+            pltpu.VMEM((ZS, TWO, TWO, TWO, *total.shape[ZS:]), F32), pltpu.VMEM(mods.shape, BF16), DMA((ZS, TWO)), DMA((ZS, TWO)), DMA((TWO,)),
         ],
         compiler_params=pltpu.CompilerParams(vmem_limit_bytes=VMEM_LIMIT), name="unpack",
-    )(total, act, weight, bias)
+    )(total, mods)
 
 
 def sinusoid(values, freq_width):
@@ -879,8 +877,8 @@
         vectors = jnp.concatenate([sums[:ZS], part_bgrad], axis=0)
         vectors = jnp.pad(vectors, ((0, 128 - vectors.shape[0]), (0, 0)))
         sources = [by_chip(g) for g in (*grads, vectors)]
-        total = reduce_all(sources, EMBED_PIECES)
-        modulation, *full = unpack(total, sources, EMBED_PIECES, cond_silu, full_wt, full_b)
+        total, modulation = reduce_all(sources, EMBED_PIECES, cond_silu, full_wt, full_b)
+        modulation, *full = unpack(total, modulation, sources, EMBED_PIECES)
         *full, sums = [g.reshape(-1, WIDTH) for g in full]
         grad_bmod = lax.dynamic_slice(sums[ZS:ZS + bgrad_rows].reshape(MOD), (SHARE * me,), (SHARE,))
         embed_grads = [g for i in range(count) for g in (full[i], sums[i], full[i + count], sums[count])]

time: 495 us -> 490 us (0.990)
  Pallas kernels: 469 us -> 459 us
    pallas_call x1, Pallas kernels: 31.8 us -> 21.1 us  [unpack(): pl.pallas_call(functools.partial(unpack_kernel, pieces), out_shape=[jax.S...]
where the time goes in v4:
time: 490 us; the launch traced here: 481 us
  Pallas kernels  459 us (94%)
  local copies, waits for them, and re-layouts  11.7 us (2%)
  other arithmetic  8.78 us (2%)
    pallas_call x1, Pallas kernels, reduce_all(): pl.pallas_call(functools.partial(reduce_kernel, pieces, split, len(source...  232 us
    pallas_call x1, Pallas kernels, scatter_sum(): pl.pallas_call(functools.partial(scatter_kernel, pieces, split, len(hidde...  133 us
    pallas_call x1, Pallas kernels, gather_blocks(): pl.pallas_call(functools.partial(gather_kernel, split, mlps), out_shape=[...  73.6 us
    pallas_call x1, Pallas kernels, unpack(): pl.pallas_call(functools.partial(unpack_kernel, pieces), out_shape=[jax.S...  21.1 us

profile of v4, /device:TPU:0, one launch (start us, length us, event | category | flops | bytes accessed | tf_op | source)
XLA Modules:
  0.0 480.8 jit_solution(16275629133095568099)
XLA Ops:
  0.6 0.7 broadcast_multiply_fusion
  1.3 0.7 broadcast_multiply_fusion.1
  2.0 2.2 fusion.4
  4.2 0.8 pad_maximum_fusion
  5.1 0.7 broadcast_in_dim.2
  5.8 1.8 fusion.1.own
  7.6 0.7 stack.21
  8.2 0.7 stack.22
  8.9 0.7 stack.23
  9.6 0.7 stack.24
  10.3 0.7 stack.25
  11.0 0.7 stack.26
  11.7 0.1 stack.27
  11.8 0.6 convert_element_type.14.biases
  12.4 73.6 %gather_wmod.1 = (bf16[4,2,2,2,184,1152]{5,4,3,2,1,0:T(8,128)(2,1)}, f32[5760,1152]{1,0:T(8,128)}, f32[1,5760]{1,0:T(1,128)}, f32[512,1152]{1,0:T(8,128)}, bf16[...) custom-call(bf16[184,1152]{1,0:T(8,128)(2,1)} %fusion.1.own, ...), custom_call_target="tpu_custom_call" | custom-call | tf_op jit(solution)/shard_map/gather_wmod/pallas_call | solution.py:649
  86.0 0.0 copy-start.2
  86.0 132.6 %scatter_wgrad.1 = (f32[184,1152]{1,0:T(8,128)}, f32[8,1152]{1,0:T(8,128)}, bf16[5760,1152]{1,0:T(8,128)(2,1)}, f32[256,1152]{1,0:T(8,128)}, f32[256,1152]{1,0:T...) custom-call(f32[4,2,2,360,1152]{4,3,2,1,0:T(8,128)} %bitcast.19, ...), custom_call_target="tpu_custom_call" | custom-call | tf_op jit(solution)/shard_map/scatter_wgrad/pallas_call | solution.py:754
  218.7 0.8 slice.23
  219.5 0.0 copy-done.2
  219.5 0.1 reduce
  219.5 0.9 select_maximum_fusion
  220.4 1.0 fusion.6
  221.4 0.8 reshape.123.refs_9_
  222.2 231.8 %reduce_embed.1 = (f32[4,2,2,2,192,1152]{5,4,3,2,1,0:T(8,128)}, bf16[512,5760]{1,0:T(8,128)(2,1)}) custom-call(f32[4,2,2,16,1152]{4,3,2,1,0:T(8,128)} %bitcast.27, f32[4,2,2,16,1152]{4,3,2,1,0:T(8,128)} %bitcast.28, f32[4,2,2,128,1152]{4,3,2,1,0:T(8,128)} %bitcast.22, f32[4,2,2,72,1152]{4,3,2,1,0:T(8,128)} %bitcast.23, f32[4,2,2,72,1152]{4,3,2,1,0:T(8,128)} %bitcast.24, ...), custom_call_target="tpu_custom_call" | custom-call | tf_op jit(solution)/shard_map/reduce_embed/pallas_call | solution.py:790
  454.0 0.0 copy-start
  454.0 21.1 %unpack.1 = (bf16[512,5760]{1,0:T(8,128)(2,1)}, f32[4,2,2,16,1152]{4,3,2,1,0:T(8,128)}, f32[4,2,2,16,1152]{4,3,2,1,0:T(8,128)}, f32[4,2,2,128,1152]{4,3,2,1,0:T(...) custom-call(f32[4,2,2,2,192,1152]{5,4,3,2,1,0:T(8,128)} %get-tuple-e, ...), custom_call_target="tpu_custom_call" | custom-call | tf_op jit(solution)/shard_map/unpack/pallas_call | solution.py:818
  475.2 0.9 slice.31
  476.1 0.6 dynamic_slice.7
  476.7 1.6 slice_reduce_fusion
  478.3 0.0 copy-start.1
  478.3 0.0 copy-done
  478.3 1.0 dynamic-slice_bitcast_fusion
  479.3 0.6 copy.35
  479.9 0.6 copy.36
  480.5 0.0 copy-done.1
  (3 shorter events, 0.0 us)
Async XLA Ops:
  86.0 133.4 %copy-start.2 = (f32[1,5760]{1,0:T(1,128)S(1)}, f32[1,5760]{1,0:T(1,128)}, u32[]{:S(2)}) copy-start(f32[1,5760]{1,0:T(1,128)} %get-tuple-element.61) | copy-start | bytes 69124
  454.0 24.3 %copy-start = (f32[184,1152]{1,0:T(8,128)S(1)}, f32[184,1152]{1,0:T(8,128)}, u32[]{:S(2)}) copy-start(f32[184,1152]{1,0:T(8,128)} %get-tuple-element.67) | copy-start | bytes 2543620
  478.3 2.2 copy-start.1
